TPU v7x, 128 devices: a whole 4x4x4 slice. The times are simulated.
128 devices in a mesh: rows: 8 (over x, y_lo), tensor: 16 (over z, y_hi, core).
Axes of the slice: x: 4, y: 4 (y_hi: 2, y_lo: 2; y = y_hi * 2 + y_lo), z: 4, core: 2. Of those that a mesh axis runs over, the one named last changes fastest.
Arguments:
- hidden: bfloat16 [2048, 28672], P('rows', 'tensor'), may hold values from -6 to 6
- down_weight: bfloat16 [28672, 8192], P('tensor', 'rows'), may hold values from -0.046875 to 0.046875
- low_feat: bfloat16 [2048, 8192], P('rows', 'tensor'), may hold values from -6 to 6
- mid_feat: bfloat16 [2048, 8192], P('rows', 'tensor'), may hold values from -6 to 6
- draft_rows: int32 [2048], replicated, may hold values from 0 to 2047, each once
- join_weight: bfloat16 [3, 8192, 8192], P(None, 'tensor', 'rows'), may hold values from -0.0390625 to 0.0390625
- cotangent: bfloat16 [2048, 8192], P('tensor', 'rows'), may hold values from -0.1796875 to 0.1796875
Outputs:
- joined: bfloat16 [2048, 8192], P('tensor', 'rows')
- join_grad: float32 [3, 8192, 8192], P(None, 'tensor', 'rows')
Inputs may be any that keep to these rules, and one draw needn't show every extreme that they name: draft_rows is a permutation of the 2048 target tokens.
All inputs are finite; a program needn't handle non-finite values.
Results may differ from a plain program's by a relative error of at most 0.0038.
Values may be sent and summed in bfloat16 or wider, within the bound.
A program may use at most 128 MiB of HBM per device.

v0:
```python
import jax
import jax.numpy as jnp
from jax import lax
from jax.sharding import Mesh
from jax.sharding import PartitionSpec as P

TENSOR = ("tensor_0", "tensor_1", "tensor_2")


def side_by_side(arrays, axis, dim, along):
    both = jnp.concatenate(arrays, axis=along)
    result, at, done = (lax.all_gather(both, axis, axis=dim, tiled=True), 0, [])
    for a in arrays:
        done.append(lax.slice_in_dim(result, at, at + a.shape[along], axis=along))
        at += a.shape[along]
    return tuple(done)


def laid_out(pieces, dim):
    pieces = jnp.moveaxis(pieces, 0, dim)
    shape = pieces.shape
    return pieces.reshape(*shape[:dim], shape[dim] * shape[dim + 1], *shape[dim + 2 :])


def piecewise(x, axis, dim, work, out_dim):
    width = x.shape[dim]
    pieces = jnp.split(x, 2, axis=dim) if width % 2 == 0 else [x]
    initial = jnp.arange(lax.axis_size(axis)) * width
    blocks = [lax.all_gather(share, axis) for share in pieces]
    made = [jax.vmap(work)(b, initial + k * (width // len(pieces))) for k, b in enumerate(blocks)]
    return laid_out(jnp.concatenate(made, axis=out_dim + 1), out_dim)


def filled_up(lines, peers):
    spare = -lines.shape[0] % peers
    if not spare:
        return lines
    return jnp.concatenate([lines, jnp.zeros((spare, *lines.shape[1:]), lines.dtype)])


def spread(x, axis, root):
    lines = jnp.where(lax.axis_index(axis) == root, x, jnp.zeros_like(x)).reshape(
        -1, *x.shape[1:][-1:]
    )
    padded = filled_up(lines, lax.axis_size(axis))
    own = lax.psum_scatter(padded, axis, scatter_dimension=0, tiled=True)
    return lax.all_gather(own, axis, axis=0, tiled=True)[: len(lines)].reshape(x.shape)


def all_blocks(x, axes, order):
    pieces = x
    for k in order:
        pieces = lax.all_gather(pieces, axes[k])
    done = order[::-1]
    back = [done.index(k) for k in range(len(axes))]
    pieces = pieces.transpose(*back, *range(len(axes), pieces.ndim))
    return pieces.reshape(-1, *x.shape)


def gather_axes(x, axes, order, dim):
    return laid_out(all_blocks(x, axes, order), dim)


def on_device(hidden, down_weight, low_feat, mid_feat, draft_rows, join_weight, cotangent):
    low_all, mid_all = side_by_side((low_feat, mid_feat), "rows", 0, 1)

    def project_rows(piece, start):
        return jnp.dot(piece, down_weight, preferred_element_type=jnp.float32)

    partial_high = piecewise(hidden, "rows", 0, project_rows, 0)
    summed = lax.psum_scatter(partial_high, TENSOR, scatter_dimension=0, tiled=True).astype(
        jnp.bfloat16
    )
    column_block = lax.all_gather(summed, TENSOR, axis=0, tiled=True)
    ratio = lax.axis_size(TENSOR) // lax.axis_size("rows")
    width = column_block.shape[1] // ratio
    tensor_index = lax.axis_index(TENSOR)
    own_cols = lax.dynamic_slice_in_dim(column_block, tensor_index % ratio * width, width, 1)
    high_all = spread(own_cols, "rows", tensor_index // ratio)
    inputs = jnp.concatenate((low_all, mid_all, high_all), axis=1)
    ordered = jnp.take(inputs, draft_rows, axis=0)
    weights = join_weight.reshape(join_weight.shape[0] * join_weight.shape[1], join_weight.shape[2])
    block = ordered
    joined = lax.psum_scatter(
        jnp.dot(block, weights, preferred_element_type=jnp.float32),
        TENSOR,
        scatter_dimension=0,
        tiled=True,
    ).astype(jnp.bfloat16)
    block = ordered
    grad_flat = lax.dot_general(
        block,
        gather_axes(cotangent, TENSOR, (1, 0, 2), 0),
        (((0,), (0,)), ((), ())),
        preferred_element_type=jnp.float32,
    )
    join_grad = grad_flat.reshape(join_weight.shape[0], join_weight.shape[1], cotangent.shape[1])
    return (joined, join_grad)


def solution(mesh):
    finer = Mesh(
        mesh.devices.reshape(mesh.shape["rows"], 4, 2, 2),
        ("rows", "tensor_0", "tensor_1", "tensor_2"),
    )
    in_specs = (
        P("rows", TENSOR),
        P(TENSOR, "rows"),
        P("rows", TENSOR),
        P("rows", TENSOR),
        P(),
        P(None, TENSOR, "rows"),
        P(TENSOR, "rows"),
    )
    out_specs = (P(TENSOR, "rows"), P(None, TENSOR, "rows"))
    return jax.shard_map(
        on_device, mesh=finer, in_specs=in_specs, out_specs=out_specs, check_vma=False
    )
```

profile of v0, /device:TPU:2, one launch (start us, length us, event | category | flops | bytes accessed | tf_op | source)
XLA Modules:
  0.0 685.2 jit_solution(2268182930426294000)
XLA Ops:
  8.1 2.3 fusion.8
  11.2 82.1 %all-gather.21.cloned.1.call-done = bf16[1024,1792]{1,0:T(8,128)(2,1)} async-done(((bf16[128,1792]{1,0:T(8,128)(2,1)}), bf16[1024,1792]{1,0:T(8,128)(2,1)}) %all-gather.21.cloned.1.call-update) | async-done | bytes 3670032 | tf_op jit(solution)/shard_map/all_gather | solution.py:29
  93.2 9.1 %fusion = f32[8,128,1024]{2,1,0:T(8,128)} fusion(bf16[8,128,1792]{2,1,0:T(8,128)(2,1)} %bitcast.32, bf16[1792,1024]{1,0:T(8,128)(2,1)} %param.8), kind=kOutput, calls=%fused_computation.4 | convolution fusion | flops 3758096384 | bytes 11534336 | tf_op jit(solution)/shard_map/vmap()/dot_general | solution.py:68
  102.4 73.4 %all-gather.19.cloned.1.call-done = bf16[1024,1792]{1,0:T(8,128)(2,1)} async-done(((bf16[128,1792]{1,0:T(8,128)(2,1)}), bf16[1024,1792]{1,0:T(8,128)(2,1)}) %all-gather.19.cloned.1.call-update) | async-done | bytes 3670032 | tf_op jit(solution)/shard_map/all_gather | solution.py:29
  175.8 7.2 %fusion.2 = f32[8,128,1024]{2,1,0:T(8,128)S(1)} fusion(bf16[8,128,1792]{2,1,0:T(8,128)(2,1)} %bitcast.33, bf16[1792,1024]{1,0:T(8,128)(2,1)} %param.8), kind=kOutput, calls=%fused_computation.6 | convolution fusion | flops 3758096384 | bytes 11534336 | tf_op jit(solution)/shard_map/vmap()/dot_general | solution.py:68
  183.0 4.1 pad_maximum_fusion
  187.2 103.5 %reduce-scatter.4.cloned.1.call-done = f32[128,1024]{1,0:T(8,128)} async-done(((f32[2048,1024]{1,0:T(8,128)}), f32[128,1024]{1,0:T(8,128)}) %reduce-scatter.4.cloned.1.call-update) | async-done | bytes 524304 | tf_op jit(solution)/shard_map/reduce_scatter | solution.py:71
  290.7 1.8 convert_element_type.6
  292.6 54.8 %all-gather.15.cloned.1.call-done = bf16[2048,1024]{1,0:T(8,128)(2,1)} async-done(((bf16[128,1024]{1,0:T(8,128)(2,1)}), bf16[2048,1024]{1,0:T(8,128)(2,1)}) %all-gather.15.cloned.1.call-update) | async-done | bytes 4194320 | tf_op jit(solution)/shard_map/all_gather | solution.py:74
  347.4 3.3 dynamic-slice_select_fusion
  350.7 15.0 %all-gather.2 = bf16[256,1024]{1,0:T(8,128)(2,1)} all-gather(bf16[128,1024]{1,0:T(8,128)(2,1)S(1)} %copy-done.3), channel_id=4, replica_groups=mesh['rows'=8,'tensor_0'=4,'tensor_1'=2,'tensor_2'=2] {'tensor_1'}, dimensions={0}, use_global_device_ids=true | all-gather | bytes 786432 | tf_op jit(solution)/shard_map/all_gather | solution.py:53
  365.8 1.9 pad_maximum_fusion.2
  367.8 32.8 %reduce-scatter.6.cloned.1.call-done = bf16[256,512]{1,0:T(8,128)(2,1)} async-done(((bf16[2048,512]{1,0:T(8,128)(2,1)}), bf16[256,512]{1,0:T(8,128)(2,1)}) %reduce-scatter.6.cloned.1.call-update) | async-done | bytes 262160 | tf_op jit(solution)/shard_map/reduce_scatter | solution.py:46
  401.7 83.4 %all-gather.13.cloned.1.call-done = bf16[2048,1024]{1,0:T(8,128)(2,1)} async-done(((bf16[256,1024]{1,0:T(8,128)(2,1)}), bf16[2048,1024]{1,0:T(8,128)(2,1)}) %all-gather.13.cloned.1.call-update) | async-done | bytes 4194320 | tf_op jit(solution)/shard_map/all_gather | solution.py:12
  485.0 52.8 %all-gather.17.cloned.1.call-done = bf16[2048,512]{1,0:T(8,128)(2,1)} async-done(((bf16[256,512]{1,0:T(8,128)(2,1)}), bf16[2048,512]{1,0:T(8,128)(2,1)}) %all-gather.17.cloned.1.call-update) | async-done | bytes 2097168 | tf_op jit(solution)/shard_map/all_gather | solution.py:47
  537.9 6.1 pad_maximum_fusion.1
  543.9 16.9 %gather_fusion = bf16[2048,1536]{1,0:T(8,128)(2,1)} fusion(bf16[2048,1536]{1,0:T(8,128)(2,1)} %pad_maximum_fusion.1, s32[2048]{0:T(1024)S(1)} %fusion.6), kind=kCustom, calls=%fused_computation | custom fusion | bytes 12591104 | tf_op jit(solution)/shard_map/jit(_take)/gather | solution.py:81
  560.8 10.8 %fusion.5 = f32[2048,1024]{1,0:T(8,128)} fusion(bf16[1536,1024]{1,0:T(8,128)(2,1)S(1)} %bitcast.25, bf16[2048,1536]{1,0:T(8,128)(2,1)} %gather_fusion, pred[2048]{0:T(1024)(128)(4,1)S(1)} %compare_and_fusion), kind=kOutput, calls=%fused_computation.9 | convolution fusion | flops 6445596672 | bytes 17827840 | tf_op jit(solution)/shard_map/dot_general | solution.py:85
  571.7 4.8 copy.13
  576.5 6.1 fusion.4
  582.7 9.0 %copy.12 = bf16[1536,2048]{1,0:T(8,128)(2,1)} copy(bf16[1536,2048]{0,1:T(8,128)(2,1)} %fusion.4) | data formatting | bytes 12582912 | tf_op jit(solution)/shard_map/jit(_take)/select_n | solution.py:81
  591.7 12.5 %fusion.9 = f32[3,512,1024]{2,1,0:T(8,128)} fusion(bf16[3,512,2048]{2,1,0:T(8,128)(2,1)} %bitcast.27, bf16[2048,1024,1]{1,0,2:T(8,128)(2,1)} %bitcast.29), kind=kOutput, calls=%fused_computation.17 | convolution fusion | flops 6442450944 | bytes 16777216 | tf_op jit(solution)/shard_map/dot_general | solution.py:91
  604.2 71.6 %reduce-scatter.8.cloned.1.call-done = f32[128,1024]{1,0:T(8,128)} async-done(((f32[2048,1024]{1,0:T(8,128)}), f32[128,1024]{1,0:T(8,128)}) %reduce-scatter.8.cloned.1.call-update) | async-done | bytes 524304 | tf_op jit(solution)/shard_map/reduce_scatter | solution.py:84
  675.9 1.8 convert_element_type.7
  (34 shorter events, 2.2 us)
Async XLA Ops:
  8.0 552.8 %copy-start = (bf16[3,512,1024]{2,1,0:T(8,128)(2,1)S(1)}, bf16[3,512,1024]{2,1,0:T(8,128)(2,1)}, u32[]{:S(2)}) copy-start(bf16[3,512,1024]{2,1,0:T(8,128)(2,1)} %param.12) | copy-start | bytes 9437188
  8.0 85.2 %all-gather.21.cloned.1.call-start = ((), (), s32[]{:S(2)}) async-start(), calls=%async_computation.10 | async-start | bytes 4128768 | tf_op jit(solution)/shard_map/all_gather | solution.py:29
  10.4 165.4 %all-gather.19.cloned.1.call-start = ((), (), s32[]{:S(2)}) async-start(), calls=%async_computation.9 | async-start | bytes 4128768 | tf_op jit(solution)/shard_map/all_gather | solution.py:29
  11.1 279.6 %reduce-scatter.4.cloned.1.call-start = ((), (), s32[]{:S(2)}) async-start(), calls=%async_computation.4 | async-start | bytes 8912896 | tf_op jit(solution)/shard_map/reduce_scatter | solution.py:71
  175.7 7.2 %copy-start.2 = (f32[8,128,1024]{2,1,0:T(8,128)S(1)}, f32[8,128,1024]{2,1,0:T(8,128)}, u32[]{:S(2)}) copy-start(f32[8,128,1024]{2,1,0:T(8,128)} %fusion) | copy-start | bytes 12582916
  187.1 163.6 %copy-start.3 = (bf16[128,1024]{1,0:T(8,128)(2,1)S(1)}, bf16[128,1024]{1,0:T(8,128)(2,1)}, u32[]{:S(2)}) copy-start(bf16[128,1024]{1,0:T(8,128)(2,1)} %param.13) | copy-start | bytes 786436
  187.2 160.2 %all-gather.15.cloned.1.call-start = ((), (), s32[]{:S(2)}) async-start(), calls=%async_computation.5 | async-start | bytes 4456448 | tf_op jit(solution)/shard_map/all_gather | solution.py:74
  292.5 108.2 %reduce-scatter.6.cloned.1.call-start = ((), (), s32[]{:S(2)}) async-start(), calls=%async_computation.6 | async-start | bytes 2359296 | tf_op jit(solution)/shard_map/reduce_scatter | solution.py:46
  350.6 51.0 %copy-start.4 = (s32[2048]{0:T(1024)S(1)}, s32[2048]{0:T(1024)}, u32[]{:S(2)}) copy-start(s32[2048]{0:T(1024)} %param.11) | copy-start | bytes 24580
  350.7 50.1 %all-gather.23.cloned.1.call-start = ((), (), s32[]{:S(2)}) async-start(), calls=%async_computation.11 | async-start | bytes 2621440 | tf_op jit(solution)/shard_map/all_gather | solution.py:53
  365.8 119.3 %all-gather.13.cloned.1.call-start = ((), (), s32[]{:S(2)}) async-start(), calls=%async_computation.3 | async-start | bytes 4718592 | tf_op jit(solution)/shard_map/all_gather | solution.py:12
  367.8 170.1 %all-gather.17.cloned.1.call-start = ((), (), s32[]{:S(2)}) async-start(), calls=%async_computation.7 | async-start | bytes 2359296 | tf_op jit(solution)/shard_map/all_gather | solution.py:47
  400.7 171.0 %all-gather.25.cloned.1.call-start = ((), (), s32[]{:S(2)}) async-start(), calls=%async_computation.12 | async-start | bytes 6291456 | tf_op jit(solution)/shard_map/all_gather | solution.py:53
  401.4 274.4 %reduce-scatter.8.cloned.1.call-start = ((), (), s32[]{:S(2)}) async-start(), calls=%async_computation.8 | async-start | bytes 8912896 | tf_op jit(solution)/shard_map/reduce_scatter | solution.py:84
  591.7 85.9 %copy-start.1 = (bf16[3,512,1024]{2,1,0:T(8,128)(2,1)S(1)}, bf16[3,512,1024]{2,1,0:T(8,128)(2,1)}, u32[]{:S(2)}) copy-start(bf16[3,512,1024]{2,1,0:T(8,128)(2,1)} %param.12) | copy-start | bytes 9437188
Sparse Core Ops, SparseCore 0:
  11.0 82.1 all-gather.20
  94.9 80.8 all-gather.18
  187.3 103.3 reduce-scatter.3
  293.6 53.7 all-gather.14
  350.8 49.8 reduce-scatter.5
  571.8 103.9 reduce-scatter.7
Sparse Core Ops, SparseCore 1:
  365.9 28.1 all-gather.22
  395.5 89.5 all-gather.12
  486.6 51.2 all-gather.16
  539.5 18.0 all-gather.24
where the time goes:
time: 686 us; the launch traced here: 685 us
  waiting for transfers between devices  556 us (81%)
  matrix products  39.7 us (6%)
  local copies, waits for them, and re-layouts  33 us (5%)
  other arithmetic  25.1 us (4%)
  between operations  15.9 us (2%)
  blocking collectives  15 us (2%)
    all_gather x2, waiting for transfers between devices, piecewise(): blocks = [lax.all_gather(share, axis) for share in pieces]  155 us
    reduce_scatter x1, waiting for transfers between devices, on_device(): lax.psum_scatter(partial_high, TENSOR, scatter_dimension=0, tiled=True)  103 us
    all_gather x1, waiting for transfers between devices, side_by_side(): result, at, done = (lax.all_gather(both, axis, axis=dim, tiled=True), 0, [])  83.4 us
    reduce_scatter x1, waiting for transfers between devices, on_device(): lax.psum_scatter(jnp.dot(block, weights, preferred_element_type=jnp.float...  71.6 us
    all_gather x1, waiting for transfers between devices, on_device(): column_block = lax.all_gather(summed, TENSOR, axis=0, tiled=True)  54.8 us
    all_gather x1, waiting for transfers between devices, spread(): lax.all_gather(own, axis, axis=0, tiled=True)[:len(lines)].reshape(x.shape)  52.8 us
    reduce_scatter x1, waiting for transfers between devices, spread(): own = lax.psum_scatter(padded, axis, scatter_dimension=0, tiled=True)  32.8 us
    gather x1, local copies, waits for them, and re-layouts, on_device(): ordered = jnp.take(inputs, draft_rows, axis=0)  16.9 us
  transfers between devices with their start and end apart: 10, of which 8 were waited for; matrix products, arithmetic and copies ran while one was open for 11% of the time, Pallas kernels for 0%

commit v1 on v0

v1 whole, which is shorter than its diff:
```python
import jax
import jax.numpy as jnp
from jax import lax
from jax.experimental import pallas as pl
from jax.experimental.pallas import tpu as pltpu
from jax.sharding import Mesh
from jax.sharding import PartitionSpec as P

AXES = ("x", "yl", "z", "yh", "c")
ROWS = ("x", "yl")
TENSOR = ("z", "yh", "c")
MESH = pl.DeviceIdType.MESH
F32, BF16 = jnp.float32, jnp.bfloat16
DX = (0, 3, 1, 0, 3, 1, 2, 2)
DY = (0, 0, 0, 1, 1, 1, 0, 1)
CUT, MID = 96, 176


def mod4(i):
    return lax.rem(i + 8, 4)


class Copies:
    def __init__(self, send_sems, recv_sems):
        self.send_sems, self.recv_sems, self.made, self.open = send_sems, recv_sems, 0, []

    def send(self, src, dst, to):
        k = self.made
        self.made += 1
        copy = pltpu.make_async_remote_copy(
            src_ref=src,
            dst_ref=dst,
            send_sem=self.send_sems.at[k],
            recv_sem=self.recv_sems.at[k],
            device_id=to,
            device_id_type=MESH,
        )
        copy.start()
        self.open.append(copy)
        return copy

    def drain(self):
        for copy in self.open:
            copy.wait_send()
        self.open = []


class RowGather:
    def __init__(self, copies, buf, src, right, left, across):
        self.send, self.buf, self.src = copies.send, buf, src
        self.right, self.left, self.across = right, left, across

    def own(self):
        b = self.buf
        self.p = self.send(self.src, b.at[3], self.across)
        self.r = self.send(self.src, b.at[1], self.right)
        self.l = self.send(self.src, b.at[2], self.left)

    def near(self):
        b = self.buf
        self.p.wait_recv()
        self.pr = self.send(b.at[3, CUT:], b.at[4, CUT:], self.right)
        self.pl = self.send(b.at[3, CUT:], b.at[5, CUT:], self.left)
        self.r.wait_recv()
        self.fr = self.send(b.at[1, :128], b.at[6, :128], self.right)
        self.yl = self.send(b.at[1, :CUT], b.at[4, :CUT], self.across)
        self.l.wait_recv()
        self.fl = self.send(b.at[2, 128:], b.at[6, 128:], self.left)
        self.yr = self.send(b.at[2, :CUT], b.at[5, :CUT], self.across)

    def far(self):
        b = self.buf
        self.pr.wait_recv()
        self.fpr = self.send(b.at[4, CUT:MID], b.at[7, CUT:MID], self.right)
        self.pl.wait_recv()
        self.fpl = self.send(b.at[5, MID:], b.at[7, MID:], self.left)

    def sides(self):
        self.yl.wait_recv()
        self.yr.wait_recv()

    def opposite(self):
        b = self.buf
        self.fr.wait_recv()
        self.yo = self.send(b.at[6, :CUT], b.at[7, :CUT], self.across)
        self.fl.wait_recv()

    def last(self):
        self.yo.wait_recv()
        self.fpr.wait_recv()
        self.fpl.wait_recv()


def kernel(
    dr_hbm, hid, w, low, mid, wj, cot,
    joined, ordered_out, cot_out,
    dr, hid_all, w4, lm_all, pq, drecv, drecv2, zr, yr, hp, high, ordered, sel, wjv,
    sb, rb, ys, yr2, cot_all, send_sems, recv_sems, high_send, high_recv, local,
):
    x, yl, z, yh, c = (lax.axis_index(a) for a in AXES)
    right, left = (mod4(x + 1), yl, z, yh, c), (mod4(x - 1), yl, z, yh, c)
    across = (x, 1 - yl, z, yh, c)
    up, down = (x, yl, mod4(z + 1), yh, c), (x, yl, mod4(z - 1), yh, c)
    far_y, core = (x, yl, z, 1 - yh, c), (x, yl, z, yh, 1 - c)
    copies = Copies(send_sems, recv_sems)
    quarter = w4.shape[2]
    half = 2 * quarter
    nlocal = [0]

    def load(src, dst):
        k = nlocal[0]
        nlocal[0] += 1
        copy = pltpu.make_async_copy(src, dst, local.at[k])
        copy.start()
        return copy

    def cb(dz, y, core_at):
        return cot_all.at[mod4(z + dz) * 4 + y * 2 + core_at]

    own_cot = cb(0, yh, c)
    cy = copies.send(cot, own_cot, far_y)
    hidden = RowGather(copies, hid_all, hid, right, left, across)
    hidden.own()
    loads = [load(hid, hid_all.at[0])]
    for j in range(4):
        at = pl.multiple_of(lax.rem(c + (1 if j < 2 else 0), 2) * half + (j % 2) * quarter, quarter)
        loads.append(load(w.at[:, pl.ds(at, quarter)], w4.at[j]))
    cot_up, cot_down, to_core = copies.send(cot, own_cot, up), copies.send(cot, own_cot, down), []
    to_core.append(copies.send(cot, own_cot, core))
    late = [load(cot, own_cot), load(low, lm_all.at[0, :, 0 : low.shape[1]])]
    late.append(load(mid, lm_all.at[0, :, low.shape[1] :]))
    late.append(load(dr_hbm, dr))
    depth = low.shape[1]
    for k in range(3):
        for d in range(2):
            late.append(
                load(wj.at[k, :, d * half : (d + 1) * half], wjv.at[d, k * depth : (k + 1) * depth])
            )
    for copy in loads:
        copy.wait()

    def project(first, stop, which):
        def body(i, _):
            s, j = first + i // 2, i % 2
            pq[which, s, j] = jnp.dot(hid_all[s], w4[which * 2 + j], preferred_element_type=F32)
            return 0

        lax.fori_loop(0, 2 * (stop - first), body, 0)

    to_pair = {}

    def product(first, stop):
        project(first, stop, 0)
        for s in range(first, stop):
            to_pair[s] = copies.send(pq.at[0, s], drecv.at[s], core)
        project(first, stop, 1)

    def pair_sum(first, stop):
        for s in range(first, stop):
            to_pair[s].wait_recv()

        def body(s, _):
            pq[1, s] = pq[1, s] + drecv[s]
            return 0

        lax.fori_loop(first, stop, body, 0)

    def chunk(k):
        return pl.ds(pl.multiple_of(mod4(k) * 64, 64), 64)

    class Sums:
        def __init__(self, group, first, stop):
            self.group, self.first, self.stop = group, first, stop

        def start(self, step):
            f, t = self.first, self.stop
            self.moved = (
                copies.send(pq.at[1, f:t, 0, chunk(z - 1 - step)], zr.at[step, 0, f:t], up),
                copies.send(pq.at[1, f:t, 1, chunk(z + 1 + step)], zr.at[step, 1, f:t], down),
            )

        def add(self, step):
            f, t = self.first, self.stop
            for d, at in ((0, chunk(z - 2 - step)), (1, chunk(z + 2 + step))):
                self.moved[d].wait_recv()
                pq[1, f:t, d, at] = pq[1, f:t, d, at] + zr[step, d, f:t]

        def advance(self, step):
            self.add(step)
            self.start(step + 1)

        def cross(self):
            self.add(2)
            f, t = self.first, self.stop
            at = pl.ds(pl.multiple_of(z * 64 + (1 - yh) * 32, 32), 32)
            self.crossed = copies.send(pq.at[1, f:t, :, at], yr.at[f:t], far_y)

        def publish(self):
            f, t, g = self.first, self.stop, self.group
            self.crossed.wait_recv()
            at = pl.ds(pl.multiple_of(z * 64 + yh * 32, 32), 32)
            for d in range(2):
                total = pq[1, f:t, d, at] + yr[f:t, d]
                hp[f:t, :, d * quarter : (d + 1) * quarter] = total.astype(BF16)
            me = z * 2 + yh
            self.sent = []
            for n in (0, 3, 1, 2, 4, 5, 6, 7):
                to = (mod4(x + DX[n]), lax.rem(yl + DY[n], 2), x, yl, c)
                copy = pltpu.make_async_remote_copy(
                    src_ref=hp.at[f:t],
                    dst_ref=high.at[f:t, me],
                    send_sem=high_send.at[g, n],
                    recv_sem=high_recv.at[g, me],
                    device_id=to,
                    device_id_type=MESH,
                )
                self.sent.append((n, copy))
                if n == 0:

                    @pl.when(jnp.logical_not(is_self))
                    def _():
                        copy.start()

                    @pl.when(is_self)
                    def _():
                        high[f:t, me] = hp[f:t]
                else:
                    copy.start()

        def arrive(self):
            f, t, g = self.first, self.stop, self.group
            for i in range(8):
                @pl.when(jnp.logical_not(jnp.logical_and(is_self, z * 2 + yh == i)))
                def _():
                    pltpu.make_async_remote_copy(
                        src_ref=hp.at[f:t],
                        dst_ref=high.at[f:t, i],
                        send_sem=high_send.at[g, 0],
                        recv_sem=high_recv.at[g, i],
                        device_id=core,
                        device_id_type=MESH,
                    ).wait_recv()

        def drain(self):
            for n, copy in self.sent:
                if n == 0:
                    pl.when(jnp.logical_not(is_self))(copy.wait_send)
                else:
                    copy.wait_send()

    is_self = jnp.logical_and(z == x, yh == yl)
    a, b, e = Sums(0, 0, 4), Sums(1, 4, 6), Sums(2, 6, 8)

    product(0, 1)
    for copy in late:
        copy.wait()
    cy.wait_recv()
    y_cot = cb(0, 1 - yh, c)
    ycot_up, ycot_down = copies.send(y_cot, y_cot, up), copies.send(y_cot, y_cot, down)
    to_core.append(copies.send(y_cot, y_cot, core))
    cot_half = cot.shape[0] // 2
    ends = []

    def cot_forward(from_down, from_up, y):
        from_down.wait_recv()
        blk = cb(-1, y, c)
        ends.append(copies.send(blk.at[:cot_half], blk.at[:cot_half], up))
        to_core.append(copies.send(blk, blk, core))
        from_up.wait_recv()
        blk = cb(1, y, c)
        ends.append(copies.send(blk.at[cot_half:], blk.at[cot_half:], down))
        to_core.append(copies.send(blk, blk, core))

    cot_forward(cot_up, cot_down, yh)

    hidden.near()
    product(1, 4)
    pair_sum(0, 4)
    a.start(0)
    hidden.far()
    a.advance(0)
    hidden.sides()
    product(4, 6)
    pair_sum(4, 6)
    b.start(0)
    a.advance(1)
    hidden.opposite()
    lowmid = RowGather(copies, lm_all, lm_all.at[0], right, left, across)
    lowmid.own()
    b.advance(0)
    product(6, 7)
    a.cross()
    b.advance(1)
    hidden.last()
    product(7, 8)
    pair_sum(6, 8)
    e.start(0)
    a.publish()
    b.cross()
    e.advance(0)
    cot_forward(ycot_up, ycot_down, 1 - yh)
    b.publish()
    e.advance(1)
    for copy in ends:
        copy.wait_recv()
    for y in (yh, 1 - yh):
        blk = cb(2, y, c)
        to_core.append(copies.send(blk, blk, core))
    e.cross()
    lowmid.near()
    e.publish()
    for copy in to_core:
        copy.wait_recv()
    cot_save = load(cot_all, cot_out)
    lowmid.far()
    lowmid.sides()
    lowmid.opposite()
    lowmid.last()

    def select(row, bx, by):
        rows = dr[pl.ds(row, 256), :]
        lane = lax.broadcasted_iota(jnp.int32, (256, 128), 1)
        for s in range(8):
            base = (mod4(bx + DX[s]) * 2 + lax.rem(by + DY[s], 2)) * 256
            rel = rows - base
            for h in range(2):
                hit = jnp.where(rel == lane + h * 128, 1.0, 0.0).astype(BF16)
                sel[:, s * 256 + h * 128 : s * 256 + (h + 1) * 128] = hit

    wide = lm_all.shape[2]

    def order_lm(i, _):
        row = pl.multiple_of(i * 256, 256)
        select(row, x, yl)
        for h in range(2):
            part = lm_all[:, :, h * depth : (h + 1) * depth].reshape(2048, depth)
            ordered[pl.ds(row, 256), h * depth : (h + 1) * depth] = jnp.dot(
                sel[...], part, preferred_element_type=F32
            ).astype(BF16)
        return 0

    lax.fori_loop(0, 8, order_lm, 0)
    saves = [load(ordered.at[:, 0:wide], ordered_out.at[:, 0:wide])]
    for g in (a, b, e):
        g.arrive()
    for g in (a, b, e):
        g.drain()
    copies.drain()

    ring_at = (mod4(z - 1), mod4(z + 1), mod4(z + 2), z)
    to_pair2 = []

    def join(i):
        base = ring_at[i] * 512

        def order_high(n, _):
            row = pl.multiple_of(base + n * 256, 256)
            select(row, z, yh)
            ordered[pl.ds(row, 256), wide:] = jnp.dot(
                sel[...], high[...].reshape(2048, half), preferred_element_type=F32
            ).astype(BF16)
            return 0

        lax.fori_loop(0, 2, order_high, 0)

        def part(which):
            side = 1 - c if which == 0 else c

            def body(d, _):
                at = pl.multiple_of(base + side * 128, 128)
                rows = jnp.concatenate(
                    [ordered[pl.ds(at, 128), :], ordered[pl.ds(at + 256, 128), :]], axis=0
                )
                value = jnp.dot(rows, wjv[d], preferred_element_type=F32)
                pq[which, 2 * i + d, 0] = value[:, :quarter]
                pq[which, 2 * i + d, 1] = value[:, quarter:]
                return 0

            lax.fori_loop(0, 2, body, 0)

        part(0)
        to_pair2.append(copies.send(pq.at[0, 2 * i : 2 * i + 2], drecv2.at[2 * i : 2 * i + 2], core))
        part(1)

    streams = (1 - yh, yh)
    turns = ((0, 2, 1, 3), (1, 2, 0, 3))

    def both(i, d, st):
        at = pl.ds(pl.multiple_of(streams[st] * 128, 128), 128)
        return pq[1, 2 * i + d, :, at] + drecv2[2 * i + d, :, at]

    moving = {}

    def turn(step, d, st):
        value = both(turns[d][step], d, st)
        if step:
            moving[step - 1, d, st].wait_recv()
            value = value + rb[d, step - 1, st].astype(F32)
        if step < 3:
            sb[d, step, st] = value.astype(BF16)
            to = up if d == 0 else down
            moving[step, d, st] = copies.send(sb.at[d, step, st], rb.at[d, step, st], to)
        return value

    join(0)
    join(1)
    to_pair2[0].wait_recv()
    turn(0, 0, 0)
    turn(0, 0, 1)
    to_pair2[1].wait_recv()
    turn(0, 1, 0)
    turn(0, 1, 1)
    join(2)
    to_pair2[2].wait_recv()
    for st in range(2):
        for d in range(2):
            turn(1, d, st)
    join(3)
    saves.append(load(ordered.at[:, wide:], ordered_out.at[:, wide:]))
    to_pair2[3].wait_recv()
    for st in range(2):
        for d in range(2):
            turn(2, d, st)
    for d in range(2):
        ys[d] = turn(3, d, 0).astype(ys.dtype)
    last = copies.send(ys, yr2, far_y)
    final = [turn(3, d, 1) for d in range(2)]
    last.wait_recv()
    for d in range(2):
        value = (final[d] + yr2[d].astype(F32)).astype(BF16)
        for h in range(2):
            at = d * half + h * quarter
            joined[:, at : at + quarter] = value[h]
    copies.drain()
    cot_save.wait()
    for copy in saves:
        copy.wait()


def on_device(hidden, down_weight, low_feat, mid_feat, draft_rows, join_weight, cotangent):
    tokens = draft_rows.shape[0]
    units, width = down_weight.shape
    depth = low_feat.shape[1]
    half, quarter = width // 2, width // 4
    dr = jnp.broadcast_to(draft_rows[:, None], (tokens, 128))
    anywhere = pl.BlockSpec(memory_space=pl.ANY)
    vmem = pltpu.VMEM
    joined, ordered, cot_all = pl.pallas_call(
        kernel,
        out_shape=(
            jax.ShapeDtypeStruct((128, width), BF16),
            jax.ShapeDtypeStruct((tokens, 3 * depth), BF16),
            jax.ShapeDtypeStruct((16, 128, width), BF16),
        ),
        in_specs=[anywhere] * 7,
        out_specs=(pl.BlockSpec(memory_space=vmem), anywhere, anywhere),
        scratch_shapes=[
            vmem((tokens, 128), jnp.int32),
            vmem((8, 256, units), BF16),
            vmem((4, units, quarter), BF16),
            vmem((8, 256, 2 * depth), BF16),
            vmem((2, 8, 2, 256, quarter), F32),
            vmem((8, 2, 256, quarter), F32),
            vmem((8, 2, 256, quarter), F32),
            vmem((3, 2, 8, 64, quarter), F32),
            vmem((8, 2, 32, quarter), F32),
            vmem((8, 32, half), BF16),
            vmem((8, 8, 32, half), BF16),
            vmem((tokens, 3 * depth), BF16),
            vmem((256, tokens), BF16),
            vmem((2, 3 * depth, half), BF16),
            vmem((2, 3, 2, 2, 128, quarter), BF16),
            vmem((2, 3, 2, 2, 128, quarter), BF16),
            vmem((2, 2, 128, quarter), BF16),
            vmem((2, 2, 128, quarter), BF16),
            vmem((16, 128, width), BF16),
            pltpu.SemaphoreType.DMA((120,)),
            pltpu.SemaphoreType.DMA((120,)),
            pltpu.SemaphoreType.DMA((3, 8)),
            pltpu.SemaphoreType.DMA((3, 8)),
            pltpu.SemaphoreType.DMA((24,)),
        ],
        compiler_params=pltpu.CompilerParams(
            has_side_effects=True, vmem_limit_bytes=66_000_000
        ),
    )(dr, hidden, down_weight, low_feat, mid_feat, join_weight, cotangent)
    grad = lax.dot_general(
        ordered,
        cot_all.reshape(tokens, width),
        (((0,), (0,)), ((), ())),
        preferred_element_type=F32,
    )
    return joined, grad.reshape(3, depth, width)


def solution(mesh):
    finer = Mesh(mesh.devices.reshape(4, 2, 4, 2, 2), AXES)
    in_specs = (
        P(ROWS, TENSOR),
        P(TENSOR, ROWS),
        P(ROWS, TENSOR),
        P(ROWS, TENSOR),
        P(),
        P(None, TENSOR, ROWS),
        P(TENSOR, ROWS),
    )
    out_specs = (P(TENSOR, ROWS), P(None, TENSOR, ROWS))
    return jax.shard_map(
        on_device, mesh=finer, in_specs=in_specs, out_specs=out_specs, check_vma=False
    )
```

time: 686 us -> 212 us (0.31)
  waiting for transfers between devices: 556 us -> 0 us
  Pallas kernels: 0 us -> 188 us
  matrix products: 39.7 us -> 11.7 us
  other arithmetic: 25.1 us -> 0 us
  local copies, waits for them, and re-layouts: 33 us -> 11.4 us
  between operations: 15.9 us -> 0.64 us
  blocking collectives: 15 us -> 0 us
    all_gather x7 -> x0, waiting for transfers between devices: 346 us -> none  [the longest x2 155 us: piecewise(): blocks = [lax.all_gather(share, axis) for share in pieces]]
    reduce_scatter x3 -> x0, waiting for transfers between devices: 208 us -> none  [the longest x1 103 us: on_device(): lax.psum_scatter(partial_high, TENSOR, scatter_dimension=0, tiled=True)]
    pallas_call x0 -> x1, Pallas kernels: none -> 188 us  [on_device(): pl.pallas_call(kernel, out_shape=(jax.ShapeDtypeStruct((128, width), BF16...]
    dot_general x4 -> x1, matrix products: 39.7 us -> 11.7 us  [on_device(): lax.dot_general(ordered, cot_all.reshape(tokens, width), (((0,), (0,)), (...]
    gather x1 -> x0, local copies, waits for them, and re-layouts: 16.9 us -> none  [on_device(): ordered = jnp.take(inputs, draft_rows, axis=0)]
    all_gather x1 -> x0, blocking collectives: 15 us -> none  [all_blocks(): pieces = lax.all_gather(pieces, axes[k])]
    concatenate x3 -> x0, other arithmetic: 12.1 us -> none  [the longest x1 6.08 us: on_device(): inputs = jnp.concatenate((low_all, mid_all, high_all), axis=1)]
    select_n x2 -> x0, other arithmetic: 9.42 us -> none  [the longest x1 6.14 us: on_device(): ordered = jnp.take(inputs, draft_rows, axis=0)]
  transfers between devices with their start and end apart: 10 -> 0, of which waited for: 8 -> 0; matrix products, arithmetic and copies ran while one was open for 11% -> 0% of each run, Pallas kernels for 0% -> 0%
where the time goes in v1:
time: 212 us
  Pallas kernels  188 us (89%)
  matrix products  11.7 us (6%)
  local copies, waits for them, and re-layouts  11.4 us (5%)
    pallas_call x1, Pallas kernels, on_device(): pl.pallas_call(kernel, out_shape=(jax.ShapeDtypeStruct((128, width), BF16...  188 us
    dot_general x1, matrix products, on_device(): lax.dot_general(ordered, cot_all.reshape(tokens, width), (((0,), (0,)), (...  11.7 us
    dot_general x1, local copies, waits for them, and re-layouts, on_device(): lax.dot_general(ordered, cot_all.reshape(tokens, width), (((0,), (0,)), (...  8.68 us

profile of v1, /device:TPU:2, one launch (start us, length us, event | category | flops | bytes accessed | tf_op | source)
XLA Modules:
  0.0 211.6 jit_solution(10547946120912490612)
XLA Ops:
  0.6 2.0 broadcast_in_dim.2.dr_hbm
  2.6 187.9 %shard_map.86 = (bf16[128,1024]{1,0:T(8,128)(2,1)}, bf16[2048,1536]{1,0:T(8,128)(2,1)}, bf16[16,128,1024]{2,1,0:T(8,128)(2,1)}) custom-call(s32[2048,128]{1,0:T(8,128)} %broadcast_in_dim.2.dr_hbm, bf16[256,1792]{1,0:T(8,128)(2,1)} %hid.1, bf16[1792,1024]{1,0:T(8,128)(2,1)} %w.1, bf16[256,512]{1,0:T(8,128)(2,1)} %low.1, bf16[256,512]{1,0:T(8,128)(2,1)} %mid.1, ...), custom_call_target="tpu_custom_call" | custom-call | tf_op jit(solution)/shard_map/pallas_call | solution.py:448
  190.6 8.7 %copy.10 = bf16[1536,2048]{1,0:T(8,128)(2,1)} copy(bf16[1536,2048]{0,1:T(8,128)(2,1)} %bitcast.7) | data formatting | bytes 12582912 | tf_op jit(solution)/shard_map/dot_general | solution.py:487
  199.2 0.0 copy-start
  199.2 11.7 %fusion = f32[3,512,1024]{2,1,0:T(8,128)} fusion(bf16[3,512,2048]{2,1,0:T(8,128)(2,1)} %bitcast.8, bf16[2048,1024,1]{1,0,2:T(8,128)(2,1)} %bitcast.9), kind=kOutput, calls=%fused_computation | convolution fusion | flops 6442450944 | bytes 16777216 | tf_op jit(solution)/shard_map/dot_general | solution.py:487
  210.9 0.0 copy-done
  210.9 0.7 copy.12
Async XLA Ops:
  199.2 11.7 %copy-start = (bf16[128,1024]{1,0:T(8,128)(2,1)S(1)}, bf16[128,1024]{1,0:T(8,128)(2,1)}, u32[]{:S(2)}) copy-start(bf16[128,1024]{1,0:T(8,128)(2,1)} %get-tuple-element.10) | copy-start | bytes 786436

commit v2 on v1

--- a/solution.py
+++ b/solution.py
@@ -13,7 +13,7 @@
 F32, BF16 = jnp.float32, jnp.bfloat16
 DX = (0, 3, 1, 0, 3, 1, 2, 2)
 DY = (0, 0, 0, 1, 1, 1, 0, 1)
-CUT, MID = 96, 176
+CUT, MID = 80, 176
 
 
 def mod4(i):
@@ -93,15 +93,27 @@
 
 def kernel(
     dr_hbm, hid, w, low, mid, wj, cot,
-    joined, ordered_out, cot_out,
-    dr, hid_all, w4, lm_all, pq, drecv, drecv2, zr, yr, hp, high, ordered, sel, wjv,
-    sb, rb, ys, yr2, cot_all, send_sems, recv_sems, high_send, high_recv, local,
+    joined, grad,
+    dr, hid_all, w4, lm_all, pq, drecv, drecv2, zr, pr, hp, high, ordered, sel, wjv,
+    sb, rb, ys, yr2, cot_all, relay, send_sems, recv_sems, pair_send, pair_recv, over_send,
+    over_recv, high_send, high_recv, local, grad_sems,
 ):
     x, yl, z, yh, c = (lax.axis_index(a) for a in AXES)
     right, left = (mod4(x + 1), yl, z, yh, c), (mod4(x - 1), yl, z, yh, c)
     across = (x, 1 - yl, z, yh, c)
     up, down = (x, yl, mod4(z + 1), yh, c), (x, yl, mod4(z - 1), yh, c)
     far_y, core = (x, yl, z, 1 - yh, c), (x, yl, z, yh, 1 - c)
+    between = (x, 1 - yl, z, 1 - yh, c)
+    is_self = z == x
+
+    barrier = pltpu.get_barrier_semaphore()
+    for to in (right, left, across, between, up, down, far_y, core):
+        pl.semaphore_signal(barrier, inc=1, device_id=to, device_id_type=MESH)
+    for n in range(4):
+        @pl.when(jnp.logical_not(jnp.logical_and(is_self, z == n)))
+        def _():
+            pl.semaphore_signal(barrier, inc=1, device_id=(z, yl, n, yh, c), device_id_type=MESH)
+    pl.semaphore_wait(barrier, jnp.where(is_self, 11, 12))
     copies = Copies(send_sems, recv_sems)
     quarter = w4.shape[2]
     half = 2 * quarter
@@ -118,7 +130,7 @@
         return cot_all.at[mod4(z + dz) * 4 + y * 2 + core_at]
 
     own_cot = cb(0, yh, c)
-    cy = copies.send(cot, own_cot, far_y)
+    cot_between = copies.send(cot, relay, between)
     hidden = RowGather(copies, hid_all, hid, right, left, across)
     hidden.own()
     loads = [load(hid, hid_all.at[0])]
@@ -191,46 +203,82 @@
 
         def cross(self):
             self.add(2)
+            f, t, g = self.first, self.stop, self.group
+            self.pair = pltpu.make_async_remote_copy(
+                src_ref=pq.at[1, f:t, :, chunk(z)],
+                dst_ref=pr.at[yh, f:t],
+                send_sem=pair_send.at[g],
+                recv_sem=pair_recv.at[g, yh],
+                device_id=(x, 1 - yl, z, yl, c),
+                device_id_type=MESH,
+            )
+            self.pair.start()
+            self.over = pltpu.make_async_remote_copy(
+                src_ref=hp.at[f:t],
+                dst_ref=hp.at[f:t],
+                send_sem=over_send.at[g],
+                recv_sem=over_recv.at[g],
+                device_id=across,
+                device_id_type=MESH,
+            )
+
+        def readers(self):
+            f, t, g = self.first, self.stop, self.group
+            made = []
+            for n in range(4):
+                made.append(
+                    pltpu.make_async_remote_copy(
+                        src_ref=hp.at[f:t],
+                        dst_ref=high.at[f:t, z],
+                        send_sem=high_send.at[g, n],
+                        recv_sem=high_recv.at[g, z],
+                        device_id=(mod4(x + n), yl, x, yh, c),
+                        device_id_type=MESH,
+                    )
+                )
+            return made
+
+        def publish(self):
             f, t = self.first, self.stop
-            at = pl.ds(pl.multiple_of(z * 64 + (1 - yh) * 32, 32), 32)
-            self.crossed = copies.send(pq.at[1, f:t, :, at], yr.at[f:t], far_y)
-
-        def publish(self):
+            made = self.readers()
+            for n in (2, 1, 3):
+                made[n].start()
+            pl.when(jnp.logical_not(is_self))(made[0].start)
+
+            @pl.when(is_self)
+            def _():
+                high[f:t, z] = hp[f:t]
+
+        def total(self):
             f, t, g = self.first, self.stop, self.group
-            self.crossed.wait_recv()
-            at = pl.ds(pl.multiple_of(z * 64 + yh * 32, 32), 32)
-            for d in range(2):
-                total = pq[1, f:t, d, at] + yr[f:t, d]
-                hp[f:t, :, d * quarter : (d + 1) * quarter] = total.astype(BF16)
-            me = z * 2 + yh
-            self.sent = []
-            for n in (0, 3, 1, 2, 4, 5, 6, 7):
-                to = (mod4(x + DX[n]), lax.rem(yl + DY[n], 2), x, yl, c)
-                copy = pltpu.make_async_remote_copy(
-                    src_ref=hp.at[f:t],
-                    dst_ref=high.at[f:t, me],
-                    send_sem=high_send.at[g, n],
-                    recv_sem=high_recv.at[g, me],
-                    device_id=to,
-                    device_id_type=MESH,
-                )
-                self.sent.append((n, copy))
-                if n == 0:
-
-                    @pl.when(jnp.logical_not(is_self))
-                    def _():
-                        copy.start()
-
-                    @pl.when(is_self)
-                    def _():
-                        high[f:t, me] = hp[f:t]
-                else:
-                    copy.start()
+
+            @pl.when(yh != yl)
+            def _():
+                for n in range(2):
+                    pltpu.make_async_remote_copy(
+                        src_ref=pr.at[n, f:t],
+                        dst_ref=pr.at[n, f:t],
+                        send_sem=pair_send.at[g],
+                        recv_sem=pair_recv.at[g, n],
+                        device_id=across,
+                        device_id_type=MESH,
+                    ).wait_recv()
+                for d in range(2):
+                    value = pr[0, f:t, d] + pr[1, f:t, d]
+                    hp[f:t, :, d * quarter : (d + 1) * quarter] = value.astype(BF16)
+                self.over.start()
+                self.publish()
+
+        def follow(self):
+            @pl.when(yh == yl)
+            def _():
+                self.over.wait_recv()
+                self.publish()
 
         def arrive(self):
             f, t, g = self.first, self.stop, self.group
-            for i in range(8):
-                @pl.when(jnp.logical_not(jnp.logical_and(is_self, z * 2 + yh == i)))
+            for i in range(4):
+                @pl.when(jnp.logical_not(jnp.logical_and(is_self, z == i)))
                 def _():
                     pltpu.make_async_remote_copy(
                         src_ref=hp.at[f:t],
@@ -242,22 +290,18 @@
                     ).wait_recv()
 
         def drain(self):
-            for n, copy in self.sent:
-                if n == 0:
-                    pl.when(jnp.logical_not(is_self))(copy.wait_send)
-                else:
-                    copy.wait_send()
-
-    is_self = jnp.logical_and(z == x, yh == yl)
+            self.pair.wait_send()
+            pl.when(yh != yl)(self.over.wait_send)
+            made = self.readers()
+            for n in (2, 1, 3):
+                made[n].wait_send()
+            pl.when(jnp.logical_not(is_self))(made[0].wait_send)
+
     a, b, e = Sums(0, 0, 4), Sums(1, 4, 6), Sums(2, 6, 8)
 
     product(0, 1)
     for copy in late:
         copy.wait()
-    cy.wait_recv()
-    y_cot = cb(0, 1 - yh, c)
-    ycot_up, ycot_down = copies.send(y_cot, y_cot, up), copies.send(y_cot, y_cot, down)
-    to_core.append(copies.send(y_cot, y_cot, core))
     cot_half = cot.shape[0] // 2
     ends = []
 
@@ -271,13 +315,21 @@
         ends.append(copies.send(blk.at[cot_half:], blk.at[cot_half:], down))
         to_core.append(copies.send(blk, blk, core))
 
+    y_cot = cb(0, 1 - yh, c)
+    cot_between.wait_recv()
+    cot_over = copies.send(relay, y_cot, across)
     cot_forward(cot_up, cot_down, yh)
 
     hidden.near()
     product(1, 4)
     pair_sum(0, 4)
     a.start(0)
+    cot_over.wait_recv()
+    ycot_up, ycot_down = copies.send(y_cot, y_cot, up), copies.send(y_cot, y_cot, down)
+    to_core.append(copies.send(y_cot, y_cot, core))
     hidden.far()
+    lowmid = RowGather(copies, lm_all, lm_all.at[0], right, left, across)
+    lowmid.own()
     a.advance(0)
     hidden.sides()
     product(4, 6)
@@ -285,37 +337,35 @@
     b.start(0)
     a.advance(1)
     hidden.opposite()
-    lowmid = RowGather(copies, lm_all, lm_all.at[0], right, left, across)
-    lowmid.own()
+    product(6, 7)
     b.advance(0)
-    product(6, 7)
     a.cross()
     b.advance(1)
     hidden.last()
     product(7, 8)
     pair_sum(6, 8)
     e.start(0)
-    a.publish()
     b.cross()
     e.advance(0)
+    lowmid.near()
+    a.total()
+    e.advance(1)
+    lowmid.far()
+    b.total()
+    a.follow()
+    e.cross()
+    lowmid.sides()
+    lowmid.opposite()
+    b.follow()
+    e.total()
+    lowmid.last()
+    e.follow()
     cot_forward(ycot_up, ycot_down, 1 - yh)
-    b.publish()
-    e.advance(1)
     for copy in ends:
         copy.wait_recv()
     for y in (yh, 1 - yh):
         blk = cb(2, y, c)
         to_core.append(copies.send(blk, blk, core))
-    e.cross()
-    lowmid.near()
-    e.publish()
-    for copy in to_core:
-        copy.wait_recv()
-    cot_save = load(cot_all, cot_out)
-    lowmid.far()
-    lowmid.sides()
-    lowmid.opposite()
-    lowmid.last()
 
     def select(row, bx, by):
         rows = dr[pl.ds(row, 256), :]
@@ -340,7 +390,42 @@
         return 0
 
     lax.fori_loop(0, 8, order_lm, 0)
-    saves = [load(ordered.at[:, 0:wide], ordered_out.at[:, 0:wide])]
+    for copy in to_core:
+        copy.wait_recv()
+
+    def saving(n, slot, part):
+        row = pl.multiple_of(lax.rem(n, depth // 256) * 256, 256)
+        return pltpu.make_async_copy(
+            drecv.at[slot * 2 + part // 2, part % 2],
+            grad.at[n // (depth // 256), pl.ds(row, 256), part * quarter : (part + 1) * quarter],
+            grad_sems.at[n, part],
+        )
+
+    def gradient(first, stop):
+        def body(n, _):
+            slot = lax.rem(n, 4)
+            features = ordered[:, pl.ds(pl.multiple_of(n * 256, 256), 256)]
+            value = lax.dot_general(
+                features,
+                cot_all[...].reshape(features.shape[0], 2 * half),
+                (((0,), (0,)), ((), ())),
+                preferred_element_type=F32,
+            )
+            for part in range(4):
+                at = part * quarter
+                drecv[slot * 2 + part // 2, part % 2] = value[:, at : at + quarter]
+            for part in range(4):
+                saving(n, slot, part).start()
+            return 0
+
+        lax.fori_loop(first, stop, body, 0)
+
+    def saved(first, stop):
+        for n in range(first, stop):
+            for part in range(4):
+                saving(n, n % 4, part).wait()
+
+    gradient(0, 4)
     for g in (a, b, e):
         g.arrive()
     for g in (a, b, e):
@@ -416,11 +501,12 @@
         for d in range(2):
             turn(1, d, st)
     join(3)
-    saves.append(load(ordered.at[:, wide:], ordered_out.at[:, wide:]))
     to_pair2[3].wait_recv()
     for st in range(2):
         for d in range(2):
             turn(2, d, st)
+    saved(0, 2)
+    gradient(4, 6)
     for d in range(2):
         ys[d] = turn(3, d, 0).astype(ys.dtype)
     last = copies.send(ys, yr2, far_y)
@@ -432,9 +518,7 @@
             at = d * half + h * quarter
             joined[:, at : at + quarter] = value[h]
     copies.drain()
-    cot_save.wait()
-    for copy in saves:
-        copy.wait()
+    saved(2, 6)
 
 
 def on_device(hidden, down_weight, low_feat, mid_feat, draft_rows, join_weight, cotangent):
@@ -445,15 +529,14 @@
     dr = jnp.broadcast_to(draft_rows[:, None], (tokens, 128))
     anywhere = pl.BlockSpec(memory_space=pl.ANY)
     vmem = pltpu.VMEM
-    joined, ordered, cot_all = pl.pallas_call(
+    joined, grad = pl.pallas_call(
         kernel,
         out_shape=(
             jax.ShapeDtypeStruct((128, width), BF16),
-            jax.ShapeDtypeStruct((tokens, 3 * depth), BF16),
-            jax.ShapeDtypeStruct((16, 128, width), BF16),
+            jax.ShapeDtypeStruct((3, depth, width), F32),
         ),
         in_specs=[anywhere] * 7,
-        out_specs=(pl.BlockSpec(memory_space=vmem), anywhere, anywhere),
+        out_specs=(pl.BlockSpec(memory_space=vmem), anywhere),
         scratch_shapes=[
             vmem((tokens, 128), jnp.int32),
             vmem((8, 256, units), BF16),
@@ -463,9 +546,9 @@
             vmem((8, 2, 256, quarter), F32),
             vmem((8, 2, 256, quarter), F32),
             vmem((3, 2, 8, 64, quarter), F32),
-            vmem((8, 2, 32, quarter), F32),
-            vmem((8, 32, half), BF16),
-            vmem((8, 8, 32, half), BF16),
+            vmem((2, 8, 2, 64, quarter), F32),
+            vmem((8, 64, half), BF16),
+            vmem((8, 4, 64, half), BF16),
             vmem((tokens, 3 * depth), BF16),
             vmem((256, tokens), BF16),
             vmem((2, 3 * depth, half), BF16),
@@ -474,23 +557,23 @@
             vmem((2, 2, 128, quarter), BF16),
             vmem((2, 2, 128, quarter), BF16),
             vmem((16, 128, width), BF16),
+            vmem((128, width), BF16),
             pltpu.SemaphoreType.DMA((120,)),
             pltpu.SemaphoreType.DMA((120,)),
-            pltpu.SemaphoreType.DMA((3, 8)),
-            pltpu.SemaphoreType.DMA((3, 8)),
+            pltpu.SemaphoreType.DMA((3,)),
+            pltpu.SemaphoreType.DMA((3, 2)),
+            pltpu.SemaphoreType.DMA((3,)),
+            pltpu.SemaphoreType.DMA((3,)),
+            pltpu.SemaphoreType.DMA((3, 4)),
+            pltpu.SemaphoreType.DMA((3, 4)),
             pltpu.SemaphoreType.DMA((24,)),
+            pltpu.SemaphoreType.DMA((6, 4)),
         ],
         compiler_params=pltpu.CompilerParams(
-            has_side_effects=True, vmem_limit_bytes=66_000_000
+            collective_id=0, has_side_effects=True, vmem_limit_bytes=66_000_000
         ),
     )(dr, hidden, down_weight, low_feat, mid_feat, join_weight, cotangent)
-    grad = lax.dot_general(
-        ordered,
-        cot_all.reshape(tokens, width),
-        (((0,), (0,)), ((), ())),
-        preferred_element_type=F32,
-    )
-    return joined, grad.reshape(3, depth, width)
+    return joined, grad
 
 
 def solution(mesh):

time: 212 us -> 192 us (0.906)
  matrix products: 11.7 us -> 0 us
  Pallas kernels: 188 us -> 181 us
    dot_general x1 -> x0, matrix products: 11.7 us -> none  [on_device(): lax.dot_general(ordered, cot_all.reshape(tokens, width), (((0,), (0,)), (...]
    dot_general x1 -> x0, local copies, waits for them, and re-layouts: 8.68 us -> none  [on_device(): lax.dot_general(ordered, cot_all.reshape(tokens, width), (((0,), (0,)), (...]
    unnamed x3 -> x2, local copies, waits for them, and re-layouts: 0.71 us -> 8.28 us
    pallas_call x1, Pallas kernels: 188 us -> 181 us  [on_device(): pl.pallas_call(kernel, out_shape=(jax.ShapeDtypeStruct((128, width), BF16...]
where the time goes in v2:
time: 192 us
  Pallas kernels  181 us (94%)
  local copies, waits for them, and re-layouts  10.3 us (5%)
    pallas_call x1, Pallas kernels, on_device(): pl.pallas_call(kernel, out_shape=(jax.ShapeDtypeStruct((128, width), BF16...  181 us
    unnamed x2, local copies, waits for them, and re-layouts  8.28 us

profile of v2, /device:TPU:2, one launch (start us, length us, event | category | flops | bytes accessed | tf_op | source)
XLA Modules:
  0.0 191.9 jit_solution(8020121427471102628)
XLA Ops:
  0.6 2.0 %broadcast_in_dim.2.dr_hbm = s32[2048,128]{1,0:T(8,128)} broadcast(s32[2048]{0:T(1024)} %param.11), dimensions={0} | broadcast | bytes 1056768 | tf_op jit(solution)/shard_map/broadcast_in_dim | solution.py:529
  2.6 181.0 %shard_map.86 = (bf16[128,1024]{1,0:T(8,128)(2,1)}, f32[3,512,1024]{2,1,0:T(8,128)}) custom-call(s32[2048,128]{1,0:T(8,128)} %broadcast_in_dim.2.dr_hbm, bf16[256,1792]{1,0:T(8,128)(2,1)} %hid.1, bf16[1792,1024]{1,0:T(8,128)(2,1)} %w.1, bf16[256,512]{1,0:T(8,128)(2,1)} %low.1, bf16[256,512]{1,0:T(8,128)(2,1)} %mid.1, bf16[3,512,1024]{2,1,0:T(8,128)(2,1)} %wj.1, ...), custom_call_target="tpu_custom_call" | custom-call | tf_op jit(solution)/shard_map/pallas_call | solution.py:532
  183.7 1.7 copy.11
  185.3 6.6 %copy.12 = f32[3,512,1024]{2,1,0:T(8,128)} copy(f32[3,512,1024]{2,1,0:T(8,128)} %get-tuple-element.5) | data formatting | bytes 12582912

commit v3 on v2

--- a/solution.py
+++ b/solution.py
@@ -13,7 +13,7 @@
 F32, BF16 = jnp.float32, jnp.bfloat16
 DX = (0, 3, 1, 0, 3, 1, 2, 2)
 DY = (0, 0, 0, 1, 1, 1, 0, 1)
-CUT, MID = 80, 176
+CUT, MID = 96, 176
 
 
 def mod4(i):
@@ -92,11 +92,11 @@
 
 
 def kernel(
-    dr_hbm, hid, w, low, mid, wj, cot,
+    rows_hbm, hid, w, low, mid, wj, cot,
     joined, grad,
-    dr, hid_all, w4, lm_all, pq, drecv, drecv2, zr, pr, hp, high, ordered, sel, wjv,
+    rows_in, dr, hid_all, w4, lm_all, pq, drecv, drecv2, zr, pr, hp, hx, high, ordered, sel, wjv,
     sb, rb, ys, yr2, cot_all, relay, send_sems, recv_sems, pair_send, pair_recv, over_send,
-    over_recv, high_send, high_recv, local, grad_sems,
+    over_recv, ring_send, ring_recv, high_send, high_recv, swap_send, swap_recv, local, grad_sems,
 ):
     x, yl, z, yh, c = (lax.axis_index(a) for a in AXES)
     right, left = (mod4(x + 1), yl, z, yh, c), (mod4(x - 1), yl, z, yh, c)
@@ -104,16 +104,13 @@
     up, down = (x, yl, mod4(z + 1), yh, c), (x, yl, mod4(z - 1), yh, c)
     far_y, core = (x, yl, z, 1 - yh, c), (x, yl, z, yh, 1 - c)
     between = (x, 1 - yl, z, 1 - yh, c)
-    is_self = z == x
+    far_z = (x, yl, mod4(z + 2), yh, c)
 
     barrier = pltpu.get_barrier_semaphore()
-    for to in (right, left, across, between, up, down, far_y, core):
+    partners = (right, left, across, between, up, down, far_z, far_y, core)
+    for to in partners:
         pl.semaphore_signal(barrier, inc=1, device_id=to, device_id_type=MESH)
-    for n in range(4):
-        @pl.when(jnp.logical_not(jnp.logical_and(is_self, z == n)))
-        def _():
-            pl.semaphore_signal(barrier, inc=1, device_id=(z, yl, n, yh, c), device_id_type=MESH)
-    pl.semaphore_wait(barrier, jnp.where(is_self, 11, 12))
+    pl.semaphore_wait(barrier, len(partners))
     copies = Copies(send_sems, recv_sems)
     quarter = w4.shape[2]
     half = 2 * quarter
@@ -141,7 +138,7 @@
     to_core.append(copies.send(cot, own_cot, core))
     late = [load(cot, own_cot), load(low, lm_all.at[0, :, 0 : low.shape[1]])]
     late.append(load(mid, lm_all.at[0, :, low.shape[1] :]))
-    late.append(load(dr_hbm, dr))
+    late.append(load(rows_hbm, rows_in))
     depth = low.shape[1]
     for k in range(3):
         for d in range(2):
@@ -222,33 +219,6 @@
                 device_id_type=MESH,
             )
 
-        def readers(self):
-            f, t, g = self.first, self.stop, self.group
-            made = []
-            for n in range(4):
-                made.append(
-                    pltpu.make_async_remote_copy(
-                        src_ref=hp.at[f:t],
-                        dst_ref=high.at[f:t, z],
-                        send_sem=high_send.at[g, n],
-                        recv_sem=high_recv.at[g, z],
-                        device_id=(mod4(x + n), yl, x, yh, c),
-                        device_id_type=MESH,
-                    )
-                )
-            return made
-
-        def publish(self):
-            f, t = self.first, self.stop
-            made = self.readers()
-            for n in (2, 1, 3):
-                made[n].start()
-            pl.when(jnp.logical_not(is_self))(made[0].start)
-
-            @pl.when(is_self)
-            def _():
-                high[f:t, z] = hp[f:t]
-
         def total(self):
             f, t, g = self.first, self.stop, self.group
 
@@ -267,18 +237,72 @@
                     value = pr[0, f:t, d] + pr[1, f:t, d]
                     hp[f:t, :, d * quarter : (d + 1) * quarter] = value.astype(BF16)
                 self.over.start()
-                self.publish()
-
-        def follow(self):
+
+        def to_reader(self, n):
+            f, t, g = self.first, self.stop, self.group
+            src = hp if n == 0 else hx.at[n - 1]
+            at = mod4(x + (0, 3, 1, 2)[n])
+            copy = pltpu.make_async_remote_copy(
+                src_ref=src.at[f:t],
+                dst_ref=high.at[f:t, z],
+                send_sem=high_send.at[g, n],
+                recv_sem=high_recv.at[g, z],
+                device_id=(x, yl, at, yh, c),
+                device_id_type=MESH,
+            )
+            return copy, at, src
+
+        def read(self, n):
+            f, t = self.first, self.stop
+            copy, at, src = self.to_reader(n)
+            pl.when(at != z)(copy.start)
+
+            @pl.when(at == z)
+            def _():
+                high[f:t, z] = src[f:t]
+
+        def ring(self, n, src, dst, to):
+            copy = pltpu.make_async_remote_copy(
+                src_ref=src,
+                dst_ref=dst,
+                send_sem=ring_send.at[self.group, n],
+                recv_sem=ring_recv.at[self.group, n],
+                device_id=to,
+                device_id_type=MESH,
+            )
+            copy.start()
+            self.rings.append(copy)
+
+        def publish(self):
+            f, t = self.first, self.stop
+
             @pl.when(yh == yl)
             def _():
                 self.over.wait_recv()
-                self.publish()
+
+            self.rings = []
+            self.ring(0, hp.at[f:t], hx.at[0, f:t], right)
+            self.ring(1, hp.at[f:t], hx.at[1, f:t], left)
+            self.read(0)
+
+        def forward(self):
+            f, t = self.first, self.stop
+            self.rings[0].wait_recv()
+            self.ring(2, hx.at[0, f:t, :32], hx.at[2, f:t, :32], right)
+            self.read(1)
+            self.rings[1].wait_recv()
+            self.ring(3, hx.at[1, f:t, 32:], hx.at[2, f:t, 32:], left)
+            self.read(2)
+
+        def finish(self):
+            self.rings[2].wait_recv()
+            self.rings[3].wait_recv()
+            self.read(3)
 
         def arrive(self):
             f, t, g = self.first, self.stop, self.group
             for i in range(4):
-                @pl.when(jnp.logical_not(jnp.logical_and(is_self, z == i)))
+                @pl.when(z != i)
                 def _():
                     pltpu.make_async_remote_copy(
                         src_ref=hp.at[f:t],
@@ -292,12 +316,14 @@
         def drain(self):
             self.pair.wait_send()
             pl.when(yh != yl)(self.over.wait_send)
-            made = self.readers()
-            for n in (2, 1, 3):
-                made[n].wait_send()
-            pl.when(jnp.logical_not(is_self))(made[0].wait_send)
-
-    a, b, e = Sums(0, 0, 4), Sums(1, 4, 6), Sums(2, 6, 8)
+            for copy in self.rings:
+                copy.wait_send()
+            for n in range(4):
+                copy, at, _ = self.to_reader(n)
+                pl.when(at != z)(copy.wait_send)
+
+    a, b, e, f = Sums(0, 0, 4), Sums(1, 4, 6), Sums(2, 6, 7), Sums(3, 7, 8)
+    groups = (a, b, e, f)
 
     product(0, 1)
     for copy in late:
@@ -315,57 +341,9 @@
         ends.append(copies.send(blk.at[cot_half:], blk.at[cot_half:], down))
         to_core.append(copies.send(blk, blk, core))
 
-    y_cot = cb(0, 1 - yh, c)
-    cot_between.wait_recv()
-    cot_over = copies.send(relay, y_cot, across)
-    cot_forward(cot_up, cot_down, yh)
-
-    hidden.near()
-    product(1, 4)
-    pair_sum(0, 4)
-    a.start(0)
-    cot_over.wait_recv()
-    ycot_up, ycot_down = copies.send(y_cot, y_cot, up), copies.send(y_cot, y_cot, down)
-    to_core.append(copies.send(y_cot, y_cot, core))
-    hidden.far()
-    lowmid = RowGather(copies, lm_all, lm_all.at[0], right, left, across)
-    lowmid.own()
-    a.advance(0)
-    hidden.sides()
-    product(4, 6)
-    pair_sum(4, 6)
-    b.start(0)
-    a.advance(1)
-    hidden.opposite()
-    product(6, 7)
-    b.advance(0)
-    a.cross()
-    b.advance(1)
-    hidden.last()
-    product(7, 8)
-    pair_sum(6, 8)
-    e.start(0)
-    b.cross()
-    e.advance(0)
-    lowmid.near()
-    a.total()
-    e.advance(1)
-    lowmid.far()
-    b.total()
-    a.follow()
-    e.cross()
-    lowmid.sides()
-    lowmid.opposite()
-    b.follow()
-    e.total()
-    lowmid.last()
-    e.follow()
-    cot_forward(ycot_up, ycot_down, 1 - yh)
-    for copy in ends:
-        copy.wait_recv()
-    for y in (yh, 1 - yh):
-        blk = cb(2, y, c)
-        to_core.append(copies.send(blk, blk, core))
+    for i in range(16):
+        lanes = jnp.broadcast_to(rows_in[i : i + 1, :], (128, 128)).astype(F32)
+        dr[i * 128 : (i + 1) * 128, :] = lanes.T.astype(jnp.int32)
 
     def select(row, bx, by):
         rows = dr[pl.ds(row, 256), :]
@@ -379,17 +357,92 @@
 
     wide = lm_all.shape[2]
 
-    def order_lm(i, _):
-        row = pl.multiple_of(i * 256, 256)
-        select(row, x, yl)
-        for h in range(2):
-            part = lm_all[:, :, h * depth : (h + 1) * depth].reshape(2048, depth)
-            ordered[pl.ds(row, 256), h * depth : (h + 1) * depth] = jnp.dot(
-                sel[...], part, preferred_element_type=F32
-            ).astype(BF16)
-        return 0
-
-    lax.fori_loop(0, 8, order_lm, 0)
+    def order_lm(first, stop):
+        def body(i, _):
+            row = pl.multiple_of(i * 256, 256)
+            select(row, x, yl)
+
+            def columns(h, _):
+                at = pl.ds(pl.multiple_of(h * depth, depth), depth)
+                ordered[pl.ds(row, 256), at] = jnp.dot(
+                    sel[...], lm_all[:, :, at].reshape(2048, depth), preferred_element_type=F32
+                ).astype(BF16)
+                return 0
+
+            lax.fori_loop(0, 2, columns, 0)
+            return 0
+
+        lax.fori_loop(first, stop, body, 0)
+
+    y_cot = cb(0, 1 - yh, c)
+    cot_between.wait_recv()
+    cot_forward(cot_up, cot_down, yh)
+
+    hidden.near()
+    product(1, 4)
+    pair_sum(0, 4)
+    a.start(0)
+    hidden.far()
+    lowmid = RowGather(copies, lm_all, lm_all.at[0], right, left, across)
+    lowmid.own()
+    a.advance(0)
+    hidden.sides()
+    product(4, 6)
+    hidden.opposite()
+    cot_over = copies.send(relay, y_cot, across)
+    pair_sum(4, 6)
+    b.start(0)
+    a.advance(1)
+    product(6, 7)
+    b.advance(0)
+    pair_sum(6, 7)
+    e.start(0)
+    a.cross()
+    b.advance(1)
+    e.advance(0)
+    hidden.last()
+    product(7, 8)
+    b.cross()
+    pair_sum(7, 8)
+    f.start(0)
+    e.advance(1)
+    lowmid.near()
+    f.advance(0)
+    e.cross()
+    cot_over.wait_recv()
+    ycot_up, ycot_down = copies.send(y_cot, y_cot, up), copies.send(y_cot, y_cot, down)
+    to_core.append(copies.send(y_cot, y_cot, core))
+    lowmid.far()
+    f.advance(1)
+    a.total()
+    lowmid.opposite()
+    f.cross()
+    b.total()
+    a.publish()
+    e.total()
+    b.publish()
+    f.total()
+    e.publish()
+    cot_forward(ycot_up, ycot_down, 1 - yh)
+    a.forward()
+    f.publish()
+    lowmid.sides()
+    lowmid.last()
+    order_lm(0, 2)
+    b.forward()
+    a.finish()
+    e.forward()
+    order_lm(2, 4)
+    f.forward()
+    b.finish()
+    e.finish()
+    f.finish()
+    order_lm(4, 8)
+    for copy in ends:
+        copy.wait_recv()
+    for y in (yh, 1 - yh):
+        blk = cb(2, y, c)
+        to_core.append(copies.send(blk, blk, core))
     for copy in to_core:
         copy.wait_recv()
 
@@ -425,47 +478,57 @@
             for part in range(4):
                 saving(n, n % 4, part).wait()
 
-    gradient(0, 4)
-    for g in (a, b, e):
+    gradient(0, 2)
+    for g in groups:
         g.arrive()
-    for g in (a, b, e):
+    for g in groups:
         g.drain()
     copies.drain()
 
     ring_at = (mod4(z - 1), mod4(z + 1), mod4(z + 2), z)
-    to_pair2 = []
-
-    def join(i):
-        base = ring_at[i] * 512
-
-        def order_high(n, _):
-            row = pl.multiple_of(base + n * 256, 256)
+
+    def order_high(i):
+        def body(n, _):
+            row = pl.multiple_of(ring_at[i] * 512 + n * 256, 256)
             select(row, z, yh)
             ordered[pl.ds(row, 256), wide:] = jnp.dot(
                 sel[...], high[...].reshape(2048, half), preferred_element_type=F32
             ).astype(BF16)
             return 0
 
-        lax.fori_loop(0, 2, order_high, 0)
-
-        def part(which):
-            side = 1 - c if which == 0 else c
-
-            def body(d, _):
-                at = pl.multiple_of(base + side * 128, 128)
-                rows = jnp.concatenate(
-                    [ordered[pl.ds(at, 128), :], ordered[pl.ds(at + 256, 128), :]], axis=0
-                )
-                value = jnp.dot(rows, wjv[d], preferred_element_type=F32)
-                pq[which, 2 * i + d, 0] = value[:, :quarter]
-                pq[which, 2 * i + d, 1] = value[:, quarter:]
-                return 0
-
-            lax.fori_loop(0, 2, body, 0)
-
-        part(0)
-        to_pair2.append(copies.send(pq.at[0, 2 * i : 2 * i + 2], drecv2.at[2 * i : 2 * i + 2], core))
-        part(1)
+        lax.fori_loop(0, 2, body, 0)
+
+    paired = {}
+
+    def join(i, d):
+        def part(which, _):
+            side = lax.rem(c + 1 - which, 2)
+            at = pl.multiple_of(ring_at[i] * 512 + side * 128, 128)
+            rows = jnp.concatenate(
+                [ordered[pl.ds(at, 128), :], ordered[pl.ds(at + 256, 128), :]], axis=0
+            )
+            value = jnp.dot(rows, wjv[d], preferred_element_type=F32)
+            pq[which, 2 * i + d, 0] = value[:, :quarter]
+            pq[which, 2 * i + d, 1] = value[:, quarter:]
+
+            @pl.when(which == 0)
+            def _():
+                swap(i, d).start()
+
+            return 0
+
+        lax.fori_loop(0, 2, part, 0)
+        paired[i, d] = swap(i, d)
+
+    def swap(i, d):
+        return pltpu.make_async_remote_copy(
+            src_ref=pq.at[0, 2 * i + d],
+            dst_ref=drecv2.at[2 * i + d],
+            send_sem=swap_send.at[i, d],
+            recv_sem=swap_recv.at[i, d],
+            device_id=core,
+            device_id_type=MESH,
+        )
 
     streams = (1 - yh, yh)
     turns = ((0, 2, 1, 3), (1, 2, 0, 3))
@@ -487,30 +550,43 @@
             moving[step, d, st] = copies.send(sb.at[d, step, st], rb.at[d, step, st], to)
         return value
 
-    join(0)
-    join(1)
-    to_pair2[0].wait_recv()
+    order_high(0)
+    join(0, 0)
+    order_high(1)
+    join(1, 1)
+    paired[0, 0].wait_recv()
     turn(0, 0, 0)
     turn(0, 0, 1)
-    to_pair2[1].wait_recv()
+    paired[1, 1].wait_recv()
     turn(0, 1, 0)
     turn(0, 1, 1)
-    join(2)
-    to_pair2[2].wait_recv()
+    order_high(2)
+    join(2, 0)
+    join(2, 1)
+    join(1, 0)
+    paired[2, 0].wait_recv()
+    paired[2, 1].wait_recv()
     for st in range(2):
         for d in range(2):
             turn(1, d, st)
-    join(3)
-    to_pair2[3].wait_recv()
+    join(0, 1)
+    order_high(3)
+    join(3, 0)
+    join(3, 1)
+    paired[1, 0].wait_recv()
+    paired[0, 1].wait_recv()
     for st in range(2):
         for d in range(2):
             turn(2, d, st)
-    saved(0, 2)
-    gradient(4, 6)
+    gradient(2, 4)
+    paired[3, 0].wait_recv()
+    paired[3, 1].wait_recv()
     for d in range(2):
         ys[d] = turn(3, d, 0).astype(ys.dtype)
     last = copies.send(ys, yr2, far_y)
     final = [turn(3, d, 1) for d in range(2)]
+    saved(0, 2)
+    gradient(4, 6)
     last.wait_recv()
     for d in range(2):
         value = (final[d] + yr2[d].astype(F32)).astype(BF16)
@@ -518,7 +594,27 @@
             at = d * half + h * quarter
             joined[:, at : at + quarter] = value[h]
     copies.drain()
+    for copy in paired.values():
+        copy.wait_send()
     saved(2, 6)
+
+
+def deliver(joined, grad, joined_out, grad_out, joined_buf, grad_buf, sems):
+    blocks = [(joined, joined_buf, joined_out)]
+    rows = grad.shape[1] // 2
+    for k in range(3):
+        for h in range(2):
+            at = (k, pl.ds(h * rows, rows))
+            blocks.append((grad.at[at], grad_buf.at[at], grad_out.at[at]))
+    loads = [pltpu.make_async_copy(s, b, sems.at[0, n]) for n, (s, b, _) in enumerate(blocks)]
+    stores = [pltpu.make_async_copy(b, o, sems.at[1, n]) for n, (_, b, o) in enumerate(blocks)]
+    for copy in loads:
+        copy.start()
+    for copy, store in zip(loads, stores):
+        copy.wait()
+        store.start()
+    for store in stores:
+        store.wait()
 
 
 def on_device(hidden, down_weight, low_feat, mid_feat, draft_rows, join_weight, cotangent):
@@ -526,7 +622,7 @@
     units, width = down_weight.shape
     depth = low_feat.shape[1]
     half, quarter = width // 2, width // 4
-    dr = jnp.broadcast_to(draft_rows[:, None], (tokens, 128))
+    rows = draft_rows.reshape(tokens // 128, 128)
     anywhere = pl.BlockSpec(memory_space=pl.ANY)
     vmem = pltpu.VMEM
     joined, grad = pl.pallas_call(
@@ -538,6 +634,7 @@
         in_specs=[anywhere] * 7,
         out_specs=(pl.BlockSpec(memory_space=vmem), anywhere),
         scratch_shapes=[
+            vmem((tokens // 128, 128), jnp.int32),
             vmem((tokens, 128), jnp.int32),
             vmem((8, 256, units), BF16),
             vmem((4, units, quarter), BF16),
@@ -548,6 +645,7 @@
             vmem((3, 2, 8, 64, quarter), F32),
             vmem((2, 8, 2, 64, quarter), F32),
             vmem((8, 64, half), BF16),
+            vmem((3, 8, 64, half), BF16),
             vmem((8, 4, 64, half), BF16),
             vmem((tokens, 3 * depth), BF16),
             vmem((256, tokens), BF16),
@@ -560,20 +658,37 @@
             vmem((128, width), BF16),
             pltpu.SemaphoreType.DMA((120,)),
             pltpu.SemaphoreType.DMA((120,)),
-            pltpu.SemaphoreType.DMA((3,)),
-            pltpu.SemaphoreType.DMA((3, 2)),
-            pltpu.SemaphoreType.DMA((3,)),
-            pltpu.SemaphoreType.DMA((3,)),
-            pltpu.SemaphoreType.DMA((3, 4)),
-            pltpu.SemaphoreType.DMA((3, 4)),
+            pltpu.SemaphoreType.DMA((4,)),
+            pltpu.SemaphoreType.DMA((4, 2)),
+            pltpu.SemaphoreType.DMA((4,)),
+            pltpu.SemaphoreType.DMA((4,)),
+            pltpu.SemaphoreType.DMA((4, 4)),
+            pltpu.SemaphoreType.DMA((4, 4)),
+            pltpu.SemaphoreType.DMA((4, 4)),
+            pltpu.SemaphoreType.DMA((4, 4)),
+            pltpu.SemaphoreType.DMA((4, 2)),
+            pltpu.SemaphoreType.DMA((4, 2)),
             pltpu.SemaphoreType.DMA((24,)),
             pltpu.SemaphoreType.DMA((6, 4)),
         ],
         compiler_params=pltpu.CompilerParams(
             collective_id=0, has_side_effects=True, vmem_limit_bytes=66_000_000
         ),
-    )(dr, hidden, down_weight, low_feat, mid_feat, join_weight, cotangent)
-    return joined, grad
+    )(rows, hidden, down_weight, low_feat, mid_feat, join_weight, cotangent)
+    return pl.pallas_call(
+        deliver,
+        out_shape=(
+            jax.ShapeDtypeStruct(joined.shape, BF16),
+            jax.ShapeDtypeStruct(grad.shape, F32),
+        ),
+        in_specs=[anywhere] * 2,
+        out_specs=(anywhere, anywhere),
+        scratch_shapes=[
+            vmem(joined.shape, BF16),
+            vmem(grad.shape, F32),
+            pltpu.SemaphoreType.DMA((2, 7)),
+        ],
+    )(joined, grad)
 
 
 def solution(mesh):

time: 192 us -> 174 us (0.906)
  local copies, waits for them, and re-layouts: 10.3 us -> 0 us
  Pallas kernels: 181 us -> 172 us
    pallas_call x1, Pallas kernels: 181 us -> 166 us  [on_device(): pl.pallas_call(kernel, out_shape=(jax.ShapeDtypeStruct((128, width), BF16...]
    unnamed x2 -> x0, local copies, waits for them, and re-layouts: 8.28 us -> none
    pallas_call x0 -> x1, Pallas kernels: none -> 5.59 us  [on_device(): pl.pallas_call(deliver, out_shape=(jax.ShapeDtypeStruct(joined.shape, BF1...]
    broadcast_in_dim x1 -> x0, local copies, waits for them, and re-layouts: 2 us -> none  [on_device(): dr = jnp.broadcast_to(draft_rows[:, None], (tokens, 128))]
where the time goes in v3:
time: 174 us; the launch traced here: 172 us
  Pallas kernels  172 us (99%)
    pallas_call x1, Pallas kernels, on_device(): pl.pallas_call(kernel, out_shape=(jax.ShapeDtypeStruct((128, width), BF16...  166 us
    pallas_call x1, Pallas kernels, on_device(): pl.pallas_call(deliver, out_shape=(jax.ShapeDtypeStruct(joined.shape, BF1...  5.59 us

profile of v3, /device:TPU:2, one launch (start us, length us, event | category | flops | bytes accessed | tf_op | source)
XLA Modules:
  0.0 172.4 jit_solution(9789596602388366929)
XLA Ops:
  0.6 166.0 %shard_map.86 = (bf16[128,1024]{1,0:T(8,128)(2,1)}, f32[3,512,1024]{2,1,0:T(8,128)}) custom-call(s32[16,128]{1,0:T(8,128)} %bitcast.1, bf16[256,1792]{1,0:T(8,128)(2,1)} %hid.1, bf16[1792,1024]{1,0:T(8,128)(2,1)} %w.1, bf16[256,512]{1,0:T(8,128)(2,1)} %low.1, bf16[256,512]{1,0:T(8,128)(2,1)} %mid.1, bf16[3,512,1024]{2,1,0:T(8,128)(2,1)} %wj.1, ...), custom_call_target="tpu_custom_call" | custom-call | tf_op jit(solution)/shard_map/pallas_call | solution.py:628
  166.7 5.6 %shard_map.87 = (bf16[128,1024]{1,0:T(8,128)(2,1)}, f32[3,512,1024]{2,1,0:T(8,128)}) custom-call(bf16[128,1024]{1,0:T(8,128)(2,1)} %get-tuple-element.4.joined, f32[3,512,1024]{2,1,0:T(8,128)} %get-tuple-element.5.grad), custom_call_target="tpu_custom_call" | custom-call | tf_op jit(solution)/shard_map/pallas_call | solution.py:678

commit v4 on v3

--- a/solution.py
+++ b/solution.py
@@ -13,7 +13,6 @@
 F32, BF16 = jnp.float32, jnp.bfloat16
 DX = (0, 3, 1, 0, 3, 1, 2, 2)
 DY = (0, 0, 0, 1, 1, 1, 0, 1)
-CUT, MID = 96, 176
 
 
 def mod4(i):
@@ -46,9 +45,10 @@
 
 
 class RowGather:
-    def __init__(self, copies, buf, src, right, left, across):
+    def __init__(self, copies, buf, src, right, left, across, cut):
         self.send, self.buf, self.src = copies.send, buf, src
         self.right, self.left, self.across = right, left, across
+        self.cut, self.mid = cut, 128 + cut // 2
 
     def own(self):
         b = self.buf
@@ -56,33 +56,39 @@
         self.r = self.send(self.src, b.at[1], self.right)
         self.l = self.send(self.src, b.at[2], self.left)
 
-    def near(self):
+    def partner(self):
+        b, cut = self.buf, self.cut
+        self.p.wait_recv()
+        self.pr = self.send(b.at[3, cut:], b.at[4, cut:], self.right)
+        self.pl = self.send(b.at[3, cut:], b.at[5, cut:], self.left)
+
+    def sideways(self):
         b = self.buf
-        self.p.wait_recv()
-        self.pr = self.send(b.at[3, CUT:], b.at[4, CUT:], self.right)
-        self.pl = self.send(b.at[3, CUT:], b.at[5, CUT:], self.left)
         self.r.wait_recv()
         self.fr = self.send(b.at[1, :128], b.at[6, :128], self.right)
-        self.yl = self.send(b.at[1, :CUT], b.at[4, :CUT], self.across)
         self.l.wait_recv()
         self.fl = self.send(b.at[2, 128:], b.at[6, 128:], self.left)
-        self.yr = self.send(b.at[2, :CUT], b.at[5, :CUT], self.across)
+
+    def over(self):
+        b, cut = self.buf, self.cut
+        self.yl = self.send(b.at[1, :cut], b.at[4, :cut], self.across)
+        self.yr = self.send(b.at[2, :cut], b.at[5, :cut], self.across)
 
     def far(self):
-        b = self.buf
+        b, cut, mid = self.buf, self.cut, self.mid
         self.pr.wait_recv()
-        self.fpr = self.send(b.at[4, CUT:MID], b.at[7, CUT:MID], self.right)
+        self.fpr = self.send(b.at[4, cut:mid], b.at[7, cut:mid], self.right)
         self.pl.wait_recv()
-        self.fpl = self.send(b.at[5, MID:], b.at[7, MID:], self.left)
+        self.fpl = self.send(b.at[5, mid:], b.at[7, mid:], self.left)
 
     def sides(self):
         self.yl.wait_recv()
         self.yr.wait_recv()
 
     def opposite(self):
-        b = self.buf
+        b, cut = self.buf, self.cut
         self.fr.wait_recv()
-        self.yo = self.send(b.at[6, :CUT], b.at[7, :CUT], self.across)
+        self.yo = self.send(b.at[6, :cut], b.at[7, :cut], self.across)
         self.fl.wait_recv()
 
     def last(self):
@@ -128,7 +134,7 @@
 
     own_cot = cb(0, yh, c)
     cot_between = copies.send(cot, relay, between)
-    hidden = RowGather(copies, hid_all, hid, right, left, across)
+    hidden = RowGather(copies, hid_all, hid, right, left, across, 96)
     hidden.own()
     loads = [load(hid, hid_all.at[0])]
     for j in range(4):
@@ -378,18 +384,20 @@
     cot_between.wait_recv()
     cot_forward(cot_up, cot_down, yh)
 
-    hidden.near()
+    hidden.partner()
+    hidden.sideways()
+    hidden.over()
+    cot_over = copies.send(relay, y_cot, across)
     product(1, 4)
     pair_sum(0, 4)
     a.start(0)
     hidden.far()
-    lowmid = RowGather(copies, lm_all, lm_all.at[0], right, left, across)
-    lowmid.own()
     a.advance(0)
     hidden.sides()
     product(4, 6)
     hidden.opposite()
-    cot_over = copies.send(relay, y_cot, across)
+    lowmid = RowGather(copies, lm_all, lm_all.at[0], right, left, across, 32)
+    lowmid.own()
     pair_sum(4, 6)
     b.start(0)
     a.advance(1)
@@ -397,33 +405,34 @@
     b.advance(0)
     pair_sum(6, 7)
     e.start(0)
+    hidden.last()
+    product(7, 8)
     a.cross()
+    pair_sum(7, 8)
+    f.start(0)
     b.advance(1)
     e.advance(0)
-    hidden.last()
-    product(7, 8)
+    f.advance(0)
+    lowmid.sideways()
     b.cross()
-    pair_sum(7, 8)
-    f.start(0)
     e.advance(1)
-    lowmid.near()
-    f.advance(0)
+    lowmid.partner()
+    f.advance(1)
     e.cross()
+    f.cross()
+    lowmid.over()
+    lowmid.opposite()
     cot_over.wait_recv()
     ycot_up, ycot_down = copies.send(y_cot, y_cot, up), copies.send(y_cot, y_cot, down)
     to_core.append(copies.send(y_cot, y_cot, core))
+    a.total()
     lowmid.far()
-    f.advance(1)
-    a.total()
-    lowmid.opposite()
-    f.cross()
     b.total()
     a.publish()
     e.total()
     b.publish()
     f.total()
     e.publish()
-    cot_forward(ycot_up, ycot_down, 1 - yh)
     a.forward()
     f.publish()
     lowmid.sides()
@@ -431,13 +440,15 @@
     order_lm(0, 2)
     b.forward()
     a.finish()
+    cot_forward(ycot_up, ycot_down, 1 - yh)
+    order_lm(2, 4)
     e.forward()
-    order_lm(2, 4)
     f.forward()
     b.finish()
+    order_lm(4, 6)
     e.finish()
     f.finish()
-    order_lm(4, 8)
+    order_lm(6, 8)
     for copy in ends:
         copy.wait_recv()
     for y in (yh, 1 - yh):
@@ -581,12 +592,16 @@
     gradient(2, 4)
     paired[3, 0].wait_recv()
     paired[3, 1].wait_recv()
-    for d in range(2):
-        ys[d] = turn(3, d, 0).astype(ys.dtype)
-    last = copies.send(ys, yr2, far_y)
+    ys[1] = turn(3, 1, 0).astype(ys.dtype)
+    relayed = copies.send(ys.at[1], yr2.at[2], between)
+    ys[0] = turn(3, 0, 0).astype(ys.dtype)
+    direct = copies.send(ys.at[0], yr2.at[0], far_y)
     final = [turn(3, d, 1) for d in range(2)]
+    relayed.wait_recv()
+    last = copies.send(yr2.at[2], yr2.at[1], across)
     saved(0, 2)
     gradient(4, 6)
+    direct.wait_recv()
     last.wait_recv()
     for d in range(2):
         value = (final[d] + yr2[d].astype(F32)).astype(BF16)
@@ -653,7 +668,7 @@
             vmem((2, 3, 2, 2, 128, quarter), BF16),
             vmem((2, 3, 2, 2, 128, quarter), BF16),
             vmem((2, 2, 128, quarter), BF16),
-            vmem((2, 2, 128, quarter), BF16),
+            vmem((3, 2, 128, quarter), BF16),
             vmem((16, 128, width), BF16),
             vmem((128, width), BF16),
             pltpu.SemaphoreType.DMA((120,)),

time: 174 us -> 179 us (1.029)
  Pallas kernels: 172 us -> 176 us
    pallas_call x1, Pallas kernels: 166 us -> 171 us  [on_device(): pl.pallas_call(kernel, out_shape=(jax.ShapeDtypeStruct((128, width), BF16...]
where the time goes in v4:
time: 179 us; the launch traced here: 177 us
  Pallas kernels  176 us (98%)
    pallas_call x1, Pallas kernels, on_device(): pl.pallas_call(kernel, out_shape=(jax.ShapeDtypeStruct((128, width), BF16...  171 us
    pallas_call x1, Pallas kernels, on_device(): pl.pallas_call(deliver, out_shape=(jax.ShapeDtypeStruct(joined.shape, BF1...  5.59 us

profile of v4, /device:TPU:2, one launch (start us, length us, event | category | flops | bytes accessed | tf_op | source)
XLA Modules:
  0.0 177.2 jit_solution(12200879593633540354)
XLA Ops:
  0.6 170.8 %shard_map.86 = (bf16[128,1024]{1,0:T(8,128)(2,1)}, f32[3,512,1024]{2,1,0:T(8,128)}) custom-call(s32[16,128]{1,0:T(8,128)} %bitcast.1, bf16[256,1792]{1,0:T(8,128)(2,1)} %hid.1, bf16[1792,1024]{1,0:T(8,128)(2,1)} %w.1, bf16[256,512]{1,0:T(8,128)(2,1)} %low.1, bf16[256,512]{1,0:T(8,128)(2,1)} %mid.1, bf16[3,512,1024]{2,1,0:T(8,128)(2,1)} %wj.1, ...), custom_call_target="tpu_custom_call" | custom-call | tf_op jit(solution)/shard_map/pallas_call | solution.py:643
  171.5 5.6 %shard_map.87 = (bf16[128,1024]{1,0:T(8,128)(2,1)}, f32[3,512,1024]{2,1,0:T(8,128)}) custom-call(bf16[128,1024]{1,0:T(8,128)(2,1)} %get-tuple-element.4.joined, f32[3,512,1024]{2,1,0:T(8,128)} %get-tuple-element.5.grad), custom_call_target="tpu_custom_call" | custom-call | tf_op jit(solution)/shard_map/pallas_call | solution.py:693

commit v5 on v4

--- a/solution.py
+++ b/solution.py
@@ -52,9 +52,11 @@
 
     def own(self):
         b = self.buf
-        self.p = self.send(self.src, b.at[3], self.across)
         self.r = self.send(self.src, b.at[1], self.right)
         self.l = self.send(self.src, b.at[2], self.left)
+
+    def own_over(self):
+        self.p = self.send(self.src, self.buf.at[3], self.across)
 
     def partner(self):
         b, cut = self.buf, self.cut
@@ -100,7 +102,7 @@
 def kernel(
     rows_hbm, hid, w, low, mid, wj, cot,
     joined, grad,
-    rows_in, dr, hid_all, w4, lm_all, pq, drecv, drecv2, zr, pr, hp, hx, high, ordered, sel, wjv,
+    rows_in, dr, hid_all, w4, low_all, mid_all, pq, drecv, drecv2, zr, pr, hp, hx, high, ordered, sel, wjv,
     sb, rb, ys, yr2, cot_all, relay, send_sems, recv_sems, pair_send, pair_recv, over_send,
     over_recv, ring_send, ring_recv, high_send, high_recv, swap_send, swap_recv, local, grad_sems,
 ):
@@ -135,6 +137,7 @@
     own_cot = cb(0, yh, c)
     cot_between = copies.send(cot, relay, between)
     hidden = RowGather(copies, hid_all, hid, right, left, across, 96)
+    hidden.own_over()
     hidden.own()
     loads = [load(hid, hid_all.at[0])]
     for j in range(4):
@@ -142,8 +145,7 @@
         loads.append(load(w.at[:, pl.ds(at, quarter)], w4.at[j]))
     cot_up, cot_down, to_core = copies.send(cot, own_cot, up), copies.send(cot, own_cot, down), []
     to_core.append(copies.send(cot, own_cot, core))
-    late = [load(cot, own_cot), load(low, lm_all.at[0, :, 0 : low.shape[1]])]
-    late.append(load(mid, lm_all.at[0, :, low.shape[1] :]))
+    late = [load(cot, own_cot), load(low, low_all.at[0]), load(mid, mid_all.at[0])]
     late.append(load(rows_hbm, rows_in))
     depth = low.shape[1]
     for k in range(3):
@@ -361,21 +363,15 @@
                 hit = jnp.where(rel == lane + h * 128, 1.0, 0.0).astype(BF16)
                 sel[:, s * 256 + h * 128 : s * 256 + (h + 1) * 128] = hit
 
-    wide = lm_all.shape[2]
-
-    def order_lm(first, stop):
+    wide = 2 * depth
+
+    def order(features, at, first, stop):
         def body(i, _):
             row = pl.multiple_of(i * 256, 256)
             select(row, x, yl)
-
-            def columns(h, _):
-                at = pl.ds(pl.multiple_of(h * depth, depth), depth)
-                ordered[pl.ds(row, 256), at] = jnp.dot(
-                    sel[...], lm_all[:, :, at].reshape(2048, depth), preferred_element_type=F32
-                ).astype(BF16)
-                return 0
-
-            lax.fori_loop(0, 2, columns, 0)
+            ordered[pl.ds(row, 256), at : at + depth] = jnp.dot(
+                sel[...], features[...].reshape(2048, depth), preferred_element_type=F32
+            ).astype(BF16)
             return 0
 
         lax.fori_loop(first, stop, body, 0)
@@ -388,16 +384,20 @@
     hidden.sideways()
     hidden.over()
     cot_over = copies.send(relay, y_cot, across)
+    lows = RowGather(copies, low_all, low_all.at[0], right, left, across, 32)
+    mids = RowGather(copies, mid_all, mid_all.at[0], right, left, across, 32)
     product(1, 4)
     pair_sum(0, 4)
     a.start(0)
     hidden.far()
+    lows.own()
+    mids.own()
     a.advance(0)
     hidden.sides()
     product(4, 6)
     hidden.opposite()
-    lowmid = RowGather(copies, lm_all, lm_all.at[0], right, left, across, 32)
-    lowmid.own()
+    lows.own_over()
+    mids.own_over()
     pair_sum(4, 6)
     b.start(0)
     a.advance(1)
@@ -405,50 +405,56 @@
     b.advance(0)
     pair_sum(6, 7)
     e.start(0)
+    a.cross()
+    b.advance(1)
+    e.advance(0)
     hidden.last()
     product(7, 8)
-    a.cross()
+    b.cross()
     pair_sum(7, 8)
     f.start(0)
-    b.advance(1)
-    e.advance(0)
+    lows.sideways()
+    lows.partner()
+    e.advance(1)
     f.advance(0)
-    lowmid.sideways()
-    b.cross()
-    e.advance(1)
-    lowmid.partner()
+    mids.sideways()
+    mids.partner()
+    e.cross()
     f.advance(1)
-    e.cross()
     f.cross()
-    lowmid.over()
-    lowmid.opposite()
     cot_over.wait_recv()
     ycot_up, ycot_down = copies.send(y_cot, y_cot, up), copies.send(y_cot, y_cot, down)
     to_core.append(copies.send(y_cot, y_cot, core))
     a.total()
-    lowmid.far()
+    a.publish()
+    lows.over()
+    lows.opposite()
+    lows.far()
     b.total()
-    a.publish()
+    b.publish()
+    mids.over()
+    mids.opposite()
+    mids.far()
+    a.forward()
     e.total()
-    b.publish()
+    e.publish()
+    b.forward()
     f.total()
-    e.publish()
-    a.forward()
     f.publish()
-    lowmid.sides()
-    lowmid.last()
-    order_lm(0, 2)
-    b.forward()
     a.finish()
+    lows.sides()
+    lows.last()
     cot_forward(ycot_up, ycot_down, 1 - yh)
-    order_lm(2, 4)
     e.forward()
+    b.finish()
+    order(low_all, 0, 0, 4)
     f.forward()
-    b.finish()
-    order_lm(4, 6)
     e.finish()
+    order(low_all, 0, 4, 8)
     f.finish()
-    order_lm(6, 8)
+    mids.sides()
+    mids.last()
+    order(mid_all, depth, 0, 8)
     for copy in ends:
         copy.wait_recv()
     for y in (yh, 1 - yh):
@@ -489,7 +495,6 @@
             for part in range(4):
                 saving(n, n % 4, part).wait()
 
-    gradient(0, 2)
     for g in groups:
         g.arrive()
     for g in groups:
@@ -592,16 +597,13 @@
     gradient(2, 4)
     paired[3, 0].wait_recv()
     paired[3, 1].wait_recv()
-    ys[1] = turn(3, 1, 0).astype(ys.dtype)
-    relayed = copies.send(ys.at[1], yr2.at[2], between)
-    ys[0] = turn(3, 0, 0).astype(ys.dtype)
-    direct = copies.send(ys.at[0], yr2.at[0], far_y)
+    for d in range(2):
+        ys[d] = turn(3, d, 0).astype(ys.dtype)
+    last = copies.send(ys, yr2, far_y)
     final = [turn(3, d, 1) for d in range(2)]
-    relayed.wait_recv()
-    last = copies.send(yr2.at[2], yr2.at[1], across)
+    gradient(0, 2)
     saved(0, 2)
     gradient(4, 6)
-    direct.wait_recv()
     last.wait_recv()
     for d in range(2):
         value = (final[d] + yr2[d].astype(F32)).astype(BF16)
@@ -653,7 +655,8 @@
             vmem((tokens, 128), jnp.int32),
             vmem((8, 256, units), BF16),
             vmem((4, units, quarter), BF16),
-            vmem((8, 256, 2 * depth), BF16),
+            vmem((8, 256, depth), BF16),
+            vmem((8, 256, depth), BF16),
             vmem((2, 8, 2, 256, quarter), F32),
             vmem((8, 2, 256, quarter), F32),
             vmem((8, 2, 256, quarter), F32),
@@ -668,7 +671,7 @@
             vmem((2, 3, 2, 2, 128, quarter), BF16),
             vmem((2, 3, 2, 2, 128, quarter), BF16),
             vmem((2, 2, 128, quarter), BF16),
-            vmem((3, 2, 128, quarter), BF16),
+            vmem((2, 2, 128, quarter), BF16),
             vmem((16, 128, width), BF16),
             vmem((128, width), BF16),
             pltpu.SemaphoreType.DMA((120,)),

time: 179 us -> 173 us (0.966)
  Pallas kernels: 176 us -> 170 us
    pallas_call x1, Pallas kernels: 171 us -> 164 us  [on_device(): pl.pallas_call(kernel, out_shape=(jax.ShapeDtypeStruct((128, width), BF16...]
where the time goes in v5:
time: 173 us; the launch traced here: 170 us
  Pallas kernels  170 us (98%)
    pallas_call x1, Pallas kernels, on_device(): pl.pallas_call(kernel, out_shape=(jax.ShapeDtypeStruct((128, width), BF16...  164 us
    pallas_call x1, Pallas kernels, on_device(): pl.pallas_call(deliver, out_shape=(jax.ShapeDtypeStruct(joined.shape, BF1...  5.59 us

profile of v5, /device:TPU:2, one launch (start us, length us, event | category | flops | bytes accessed | tf_op | source)
XLA Modules:
  0.0 170.4 jit_solution(3956180160535336219)
XLA Ops:
  0.6 164.0 %shard_map.86 = (bf16[128,1024]{1,0:T(8,128)(2,1)}, f32[3,512,1024]{2,1,0:T(8,128)}) custom-call(s32[16,128]{1,0:T(8,128)} %bitcast.1, bf16[256,1792]{1,0:T(8,128)(2,1)} %hid.1, bf16[1792,1024]{1,0:T(8,128)(2,1)} %w.1, bf16[256,512]{1,0:T(8,128)(2,1)} %low.1, bf16[256,512]{1,0:T(8,128)(2,1)} %mid.1, bf16[3,512,1024]{2,1,0:T(8,128)(2,1)} %wj.1, ...), custom_call_target="tpu_custom_call" | custom-call | tf_op jit(solution)/shard_map/pallas_call | solution.py:645
  164.6 5.6 %shard_map.87 = (bf16[128,1024]{1,0:T(8,128)(2,1)}, f32[3,512,1024]{2,1,0:T(8,128)}) custom-call(bf16[128,1024]{1,0:T(8,128)(2,1)} %get-tuple-element.4.joined, f32[3,512,1024]{2,1,0:T(8,128)} %get-tuple-element.5.grad), custom_call_target="tpu_custom_call" | custom-call | tf_op jit(solution)/shard_map/pallas_call | solution.py:696

commit v6 on v5

--- a/solution.py
+++ b/solution.py
@@ -618,9 +618,9 @@
 
 def deliver(joined, grad, joined_out, grad_out, joined_buf, grad_buf, sems):
     blocks = [(joined, joined_buf, joined_out)]
-    rows = grad.shape[1] // 2
+    rows = grad.shape[1] // 4
     for k in range(3):
-        for h in range(2):
+        for h in range(4):
             at = (k, pl.ds(h * rows, rows))
             blocks.append((grad.at[at], grad_buf.at[at], grad_out.at[at]))
     loads = [pltpu.make_async_copy(s, b, sems.at[0, n]) for n, (s, b, _) in enumerate(blocks)]
@@ -704,7 +704,7 @@
         scratch_shapes=[
             vmem(joined.shape, BF16),
             vmem(grad.shape, F32),
-            pltpu.SemaphoreType.DMA((2, 7)),
+            pltpu.SemaphoreType.DMA((2, 13)),
         ],
     )(joined, grad)
 

time: 173 us -> 173 us (level)
  no operation moved by 1% of the time
where the time goes in v6:
time: 173 us; the launch traced here: 170 us
  Pallas kernels  169 us (98%)
    pallas_call x1, Pallas kernels, on_device(): pl.pallas_call(kernel, out_shape=(jax.ShapeDtypeStruct((128, width), BF16...  164 us
    pallas_call x1, Pallas kernels, on_device(): pl.pallas_call(deliver, out_shape=(jax.ShapeDtypeStruct(joined.shape, BF1...  5.49 us

profile of v6, /device:TPU:2, one launch (start us, length us, event | category | flops | bytes accessed | tf_op | source)
XLA Modules:
  0.0 170.3 jit_solution(12440939142076761251)
XLA Ops:
  0.6 164.0 %shard_map.86 = (bf16[128,1024]{1,0:T(8,128)(2,1)}, f32[3,512,1024]{2,1,0:T(8,128)}) custom-call(s32[16,128]{1,0:T(8,128)} %bitcast.1, bf16[256,1792]{1,0:T(8,128)(2,1)} %hid.1, bf16[1792,1024]{1,0:T(8,128)(2,1)} %w.1, bf16[256,512]{1,0:T(8,128)(2,1)} %low.1, bf16[256,512]{1,0:T(8,128)(2,1)} %mid.1, bf16[3,512,1024]{2,1,0:T(8,128)(2,1)} %wj.1, ...), custom_call_target="tpu_custom_call" | custom-call | tf_op jit(solution)/shard_map/pallas_call | solution.py:645
  164.6 5.5 %shard_map.87 = (bf16[128,1024]{1,0:T(8,128)(2,1)}, f32[3,512,1024]{2,1,0:T(8,128)}) custom-call(bf16[128,1024]{1,0:T(8,128)(2,1)} %get-tuple-element.4.joined, f32[3,512,1024]{2,1,0:T(8,128)} %get-tuple-element.5.grad), custom_call_target="tpu_custom_call" | custom-call | tf_op jit(solution)/shard_map/pallas_call | solution.py:696
